TPU v7x, 32 devices: a 4x4x1 block of a 4x4x8 slice. The times are simulated.
32 devices in a mesh: dp: 1 (over z), cp: 32 (over y, x, core).
Axes of the slice: x: 4, y: 4, z: 1, core: 2. Of those that a mesh axis runs over, the one named last changes fastest.
The devices are a block of a 4x4x8 slice.
Arguments:
- x: bfloat16 [8, 6144], P('dp')
- w_dq: bfloat16 [6144, 1536], replicated
- g_q: float32 [1536], replicated
- w_uq: bfloat16 [1536, 12288], replicated
- w_dkv: bfloat16 [6144, 576], replicated
- g_kv: float32 [512], replicated
- w_uk: bfloat16 [512, 64, 128], replicated
- w_uv: bfloat16 [512, 64, 128], replicated
- w_o: bfloat16 [8192, 6144], replicated
- cache_c: bfloat16 [8, 65536, 512], P('dp', 'cp')
- cache_kr: bfloat16 [8, 65536, 64], P('dp', 'cp')
- ctx_len: int32 [8], P('dp')
Outputs:
- output 1: bfloat16 [8, 6144], P('dp')
- output 2: bfloat16 [8, 512], P('dp')
- output 3: bfloat16 [8, 64], P('dp')
All inputs are finite; a program needn't handle non-finite values.
Results may differ from a plain program's by a relative error of at most 0.00615798.
Values sent between devices are 32-bit elements.
A program may use at most 768 MiB of HBM per device.

v0:
```python
import jax
import jax.numpy as jnp
from jax import lax
from jax.sharding import PartitionSpec as P, NamedSharding

NORM_EPS = 1e-6
ROPE_THETA = 10000.0
MASKED = -1e30


def rms_norm(values, gain_vec):
    mean_sq = jnp.mean(jnp.square(values), axis=-1, keepdims=True)
    return values * lax.rsqrt(mean_sq + NORM_EPS) * gain_vec


def rope_tables(positions, rope_dim):
    half_dim = rope_dim // 2
    inv_freq = ROPE_THETA ** (-2.0 * jnp.arange(half_dim, dtype=jnp.float32) / rope_dim)
    angles = positions.astype(jnp.float32)[..., None] * inv_freq
    return jnp.cos(angles), jnp.sin(angles)


def rope_rotate(values, cos_tab, sin_tab):
    half_dim = values.shape[-1] // 2
    lo_half = values[..., :half_dim]
    hi_half = values[..., half_dim:]
    return jnp.concatenate([lo_half * cos_tab - hi_half * sin_tab, hi_half * cos_tab + lo_half * sin_tab], axis=-1)


def project_step(x, w_dq, g_q, w_uq, w_dkv, g_kv, w_uk, ctx_len):
    n_req = x.shape[0]
    latent, n_heads, nope_dim = w_uk.shape
    rope_dim = w_dkv.shape[1] - latent
    cq_low = jnp.dot(x, w_dq, preferred_element_type=jnp.float32).astype(jnp.bfloat16)
    cq_norm = rms_norm(cq_low.astype(jnp.float32), g_q).astype(jnp.bfloat16)
    q_full = jnp.dot(cq_norm, w_uq, preferred_element_type=jnp.float32).astype(jnp.bfloat16)
    q_full = q_full.reshape(n_req, n_heads, nope_dim + rope_dim)
    cos_tab, sin_tab = rope_tables(ctx_len, rope_dim)
    q_rope = rope_rotate(q_full[:, :, nope_dim:].astype(jnp.float32), cos_tab[:, None, :], sin_tab[:, None, :]).astype(jnp.bfloat16)
    q_lat = jnp.einsum('bhn,khn->bhk', q_full[:, :, :nope_dim], w_uk, preferred_element_type=jnp.float32).astype(jnp.bfloat16)
    kv_full = jnp.dot(x, w_dkv, preferred_element_type=jnp.float32)
    c_new = rms_norm(kv_full[:, :latent], g_kv).astype(jnp.bfloat16)
    kr_new = rope_rotate(kv_full[:, latent:], cos_tab, sin_tab).astype(jnp.bfloat16)
    return q_lat, q_rope, c_new, kr_new


def block_partials(q_lat, q_rope, c_new, kr_new, cache_c, cache_kr, ctx_len, shard_idx, score_scale):
    t_dev = cache_c.shape[1]
    scores = (jnp.einsum('bhk,btk->bht', q_lat, cache_c, preferred_element_type=jnp.float32)
              + jnp.einsum('bhr,btr->bht', q_rope, cache_kr, preferred_element_type=jnp.float32)) * score_scale
    positions = shard_idx * t_dev + jnp.arange(t_dev)
    valid_pos = positions[None, None, :] < ctx_len[:, None, None]
    scores = jnp.where(valid_pos, scores, MASKED)
    is_owner = ((ctx_len // t_dev) == shard_idx)[:, None]
    new_score = (jnp.einsum('bhk,bk->bh', q_lat, c_new, preferred_element_type=jnp.float32)
                 + jnp.einsum('bhr,br->bh', q_rope, kr_new, preferred_element_type=jnp.float32)) * score_scale
    new_score = jnp.where(is_owner, new_score, MASKED)
    row_max = jnp.maximum(jnp.max(scores, axis=2), new_score)
    weights = jnp.where(valid_pos, jnp.exp(scores - row_max[:, :, None]), 0.0)
    new_weight = jnp.where(is_owner, jnp.exp(new_score - row_max), 0.0)
    row_sum = jnp.sum(weights, axis=2) + new_weight
    lat_acc = jnp.einsum('bht,btk->bhk', weights.astype(jnp.bfloat16), cache_c, preferred_element_type=jnp.float32)
    lat_acc = lat_acc + new_weight.astype(jnp.bfloat16).astype(jnp.float32)[:, :, None] * c_new.astype(jnp.float32)[:, None, :]
    return row_max, row_sum, lat_acc


def output_step(x, o_lat, w_uv, w_o):
    o_heads = jnp.einsum('bhk,khv->bhv', o_lat, w_uv, preferred_element_type=jnp.float32).astype(jnp.bfloat16)
    attn_out = jnp.dot(o_heads.reshape(x.shape[0], -1), w_o, preferred_element_type=jnp.float32)
    return (x.astype(jnp.float32) + attn_out).astype(jnp.bfloat16)


def solution(mesh):
    def decode_step(x, w_dq, g_q, w_uq, w_dkv, g_kv, w_uk, w_uv, w_o, cache_c, cache_kr, ctx_len):
        score_scale = (w_uk.shape[2] + cache_kr.shape[2]) ** -0.5
        shard_idx = lax.axis_index('cp')
        q_lat, q_rope, c_new, kr_new = project_step(x, w_dq, g_q, w_uq, w_dkv, g_kv, w_uk, ctx_len)
        row_max, row_sum, lat_acc = block_partials(q_lat, q_rope, c_new, kr_new, cache_c, cache_kr, ctx_len, shard_idx, score_scale)
        packed = jnp.concatenate([row_max[:, :, None], row_sum[:, :, None], lat_acc], axis=2)
        gathered = lax.all_gather(packed, 'cp')
        block_max = gathered[:, :, :, 0]
        glob_max = jnp.max(block_max, axis=0)
        factor = jnp.exp(block_max - glob_max[None])
        mass_sum = jnp.sum(factor * gathered[:, :, :, 1], axis=0)
        lat_sum = jnp.sum(factor[:, :, :, None] * gathered[:, :, :, 2:], axis=0)
        o_lat = (lat_sum / mass_sum[:, :, None]).astype(jnp.bfloat16)
        return output_step(x, o_lat, w_uv, w_o), c_new, kr_new

    spec_rows = P('dp', None)
    spec_cache = P('dp', 'cp', None)
    in_specs = (spec_rows, P(), P(), P(), P(), P(), P(), P(), P(), spec_cache, spec_cache, P('dp'))
    out_specs = (spec_rows, spec_rows, spec_rows)
    return jax.shard_map(decode_step, mesh=mesh, in_specs=in_specs, out_specs=out_specs, check_vma=False)
```

profile of v0, /device:TPU:97, one launch (start us, length us, event | category | flops | bytes accessed | tf_op | source)
XLA Modules:
  0.0 366.7 jit_solution(916227516092690732)
XLA Ops:
  7.3 8.0 %multiply_reduce_fusion = (f32[8]{0:T(128)S(1)}, f32[8,1536]{1,0:T(8,128)S(1)}) fusion(bf16[8,6144]{1,0:T(8,128)(2,1)} %param.12, bf16[6144,1536]{1,0:T(8,128)(2,1)} %param.13), kind=kOutput, calls=%fused_computation.44 | convolution fusion | flops 151044096 | bytes 19021856 | tf_op jit(solution)/shard_map/dot_general | solution.py:34
  15.3 14.5 %convolution_convert_fusion = bf16[8,12288]{1,0:T(8,128)(2,1)S(1)} fusion(bf16[1536,12288]{1,0:T(8,128)(2,1)} %param.15, f32[8,1536]{1,0:T(8,128)S(1)} %get-tuple-element.14, f32[1536]{0:T(1024)S(1)} %copy-done.4, f32[8]{0:T(128)S(1)} %add_rsqrt_fusion.1), kind=kOutput, calls=%fused_computation.2 | convolution fusion | flops 302125056 | bytes 38000672 | tf_op jit(solution)/shard_map/dot_general | solution.py:36
  29.9 0.3 reshape.119
  30.4 4.9 %fusion.53 = f32[8,576]{1,0:T(8,128)S(1)} fusion(bf16[8,6144]{1,0:T(8,128)(2,1)S(1)} %copy-done.3, bf16[6144,576]{0,1:T(8,128)(2,1)} %param.16), kind=kOutput, calls=%fused_computation.77 | convolution fusion | flops 56623104 | bytes 7194624 | tf_op jit(solution)/shard_map/dot_general | solution.py:41
  35.5 20.7 %fusion.20 = bf16[8,64,512]{2,0,1:T(8,128)(2,1)S(1)} fusion(bf16[512,64,128]{2,1,0:T(8,128)(2,1)} %param.18, bf16[8,64,128]{2,1,0:T(8,128)(2,1)S(1)} %slice.43), kind=kOutput, calls=%fused_computation.22 | convolution fusion | flops 67371008 | bytes 9043968 | tf_op jit(solution)/shard_map/bhn,khn->bhk/dot_general | solution.py:40
  56.2 0.3 fusion.33
  56.5 12.8 %fusion.35 = f32[8,64,2048]{2,1,0:T(8,128)} fusion(bf16[8,2048,512]{2,1,0:T(8,128)(2,1)} %param.21, bf16[8,64,512]{2,0,1:T(8,128)(2,1)S(1)} %fusion.20), kind=kOutput, calls=%fused_computation.29 | convolution fusion | flops 1073741824 | bytes 21495808 | tf_op jit(solution)/shard_map/bhk,btk->bht/dot_general | solution.py:49
  69.7 0.2 fusion.43
  69.9 3.5 fusion.52
  73.5 1.8 copy-done.2
  75.3 1.2 fusion.7
  76.6 0.2 copy.40
  77.0 10.1 %fusion.14 = f32[8,64,512]{2,1,0:T(8,128)S(1)} fusion(bf16[8,2048,512]{2,1,0:T(8,128)(2,1)} %param.21, f32[8,64,2048]{2,1,0:T(8,128)} %copy-done.2, f32[8,64]{1,0:T(8,128)S(1)} %fusion.47, pred[8,2048]{1,0:T(8,128)(4,1)S(1)} %broadcast_compare_fusion, f32[8,512]{1,0:T(8,128)S(1)} %get-tuple-element.5, f32[8,64]{1,0:T(8,128)S(1)} %convert_element_type.102), kind=kOutput, calls=%fused_computation.20 | convolution fusion | flops 1077411840 | bytes 22056960 | tf_op jit(solution)/shard_map/bht,btk->bhk/dot_general | solution.py:62
  87.1 1.6 pad_maximum_fusion
  88.8 0.7 pad_maximum_fusion.4
  89.4 134.1 %all-gather.3.cloned.1.call-done = f32[256,64,514]{2,1,0:T(8,128)} async-done(((f32[8,64,514]{2,1,0:T(8,128)}), f32[256,64,514]{2,1,0:T(8,128)}) %all-gather.3.cloned.1.call-update) | async-done | bytes 33685520 | tf_op jit(solution)/shard_map/all_gather | solution.py:80
  223.6 70.8 %copy.41 = f32[256,64,514]{1,0,2:T(8,128)} copy(f32[256,64,514]{2,1,0:T(8,128)} %all-gather.3.cloned.1.call-done) | data formatting | bytes 67371008 | tf_op jit(solution)/shard_map/all_gather | solution.py:80
  294.3 0.9 slice_reduce_fusion
  295.3 1.0 fusion.38
  296.3 0.9 exponential_bitcast_fusion
  297.2 21.5 %fusion = f32[8,64,512]{1,0,2:T(8,128)S(1)} fusion(f32[32,8,64,514]{2,1,0,3:T(8,128)} %bitcast.9, f32[32,8,64]{2,1,0:T(8,128)S(1)} %exponential_bitcast_fusion), kind=kLoop, calls=%fused_computation.1 | loop fusion | flops 16515072 | bytes 34668544 | tf_op jit(solution)/shard_map/reduce_sum | solution.py:85
  318.7 0.7 copy.49
  319.4 0.9 divide_convert_fusion
  320.3 39.1 %fusion.5 = bf16[8,6144]{1,0:T(8,128)(2,1)} fusion(bf16[8192,6144]{1,0:T(8,128)(2,1)} %param.20, bf16[512,64,128]{2,1,0:T(8,128)(2,1)} %param.19, bf16[8,64,512]{2,1,0:T(8,128)(2,1)} %divide_convert_fusion, bf16[8,6144]{1,0:T(8,128)(2,1)S(1)} %copy-done.3), kind=kOutput, calls=%fused_computation.8 | convolution fusion | flops 872628224 | bytes 109772800 | tf_op jit(solution)/shard_map/dot_general | solution.py:69
  (35 shorter events, 1.2 us)
Async XLA Ops:
  7.2 62.7 %copy-start = (bf16[8,2048,64]{1,2,0:T(8,128)(2,1)S(1)}, bf16[8,2048,64]{1,2,0:T(8,128)(2,1)}, u32[]{:S(2)}) copy-start(bf16[8,2048,64]{1,2,0:T(8,128)(2,1)} %param.22) | copy-start | bytes 6291460
  7.2 216.4 %all-gather.3.cloned.1.call-start = ((), (), s32[]{:S(2)}) async-start(), calls=%async_computation | async-start | bytes 43253760 | tf_op jit(solution)/shard_map/all_gather | solution.py:80
  7.3 8.0 %copy-start.4 = (f32[1536]{0:T(1024)S(1)}, f32[1536]{0:T(1024)}, u32[]{:S(2)}) copy-start(f32[1536]{0:T(1024)} %param.14) | copy-start | bytes 18436
  15.3 14.9 %copy-start.7 = (s32[8]{0:T(128)S(1)}, s32[8]{0:T(128)}, u32[]{:S(2)}) copy-start(s32[8]{0:T(128)} %param.23) | copy-start | bytes 100
  15.3 15.1 %copy-start.3 = (bf16[8,6144]{1,0:T(8,128)(2,1)S(1)}, bf16[8,6144]{1,0:T(8,128)(2,1)}, u32[]{:S(2)}) copy-start(bf16[8,6144]{1,0:T(8,128)(2,1)} %param.12) | copy-start | bytes 294916
  29.8 5.6 %copy-start.6 = (f32[512]{0:T(512)S(1)}, f32[512]{0:T(512)}, u32[]{:S(2)}) copy-start(f32[512]{0:T(512)} %param.17) | copy-start | bytes 6148
  35.5 33.8 %copy-start.5 = (bf16[8,512]{1,0:T(8,128)(2,1)}, bf16[8,512]{1,0:T(8,128)(2,1)S(1)}, u32[]{:S(2)}) copy-start(bf16[8,512]{1,0:T(8,128)(2,1)S(1)} %get-tuple-element.6) | copy-start | bytes 24580
  73.4 1.9 copy-start.2
  320.3 39.1 %copy-start.1 = (bf16[8,2048,64]{1,2,0:T(8,128)(2,1)S(1)}, bf16[8,2048,64]{1,2,0:T(8,128)(2,1)}, u32[]{:S(2)}) copy-start(bf16[8,2048,64]{1,2,0:T(8,128)(2,1)} %param.22) | copy-start | bytes 6291460
Sparse Core Ops, SparseCore 0:
  88.9 134.6 all-gather.2
where the time goes:
time: 372 us; the launch traced here: 367 us
  waiting for transfers between devices  134 us (36%)
  matrix products  114 us (31%)
  local copies, waits for them, and re-layouts  74 us (20%)
  other arithmetic  29.6 us (8%)
  between operations  14.7 us (4%)
    all_gather x1, waiting for transfers between devices, decode_step(): gathered = lax.all_gather(packed, 'cp')  134 us
    all_gather x1, local copies, waits for them, and re-layouts, decode_step(): gathered = lax.all_gather(packed, 'cp')  70.8 us
    dot_general x1, matrix products, output_step(): jnp.dot(o_heads.reshape(x.shape[0], -1), w_o, preferred_element_type=jnp....  39.1 us
    reduce_sum x1, other arithmetic, decode_step(): lat_sum = jnp.sum(factor[:, :, :, None] * gathered[:, :, :, 2:], axis=0)  21.5 us
    dot_general x1, matrix products, project_step(): jnp.einsum('bhn,khn->bhk', q_full[:, :, :nope_dim], w_uk, preferred_eleme...  20.7 us
    dot_general x1, matrix products, project_step(): jnp.dot(cq_norm, w_uq, preferred_element_type=jnp.float32)  14.5 us
    dot_general x1, matrix products, block_partials(): jnp.einsum('bhk,btk->bht', q_lat, cache_c, preferred_element_type=jnp.flo...  12.8 us
    dot_general x1, matrix products, block_partials(): jnp.einsum('bht,btk->bhk', weights.astype(jnp.bfloat16), cache_c, preferr...  10.1 us
  transfers between devices with their start and end apart: 1, of which 1 were waited for; matrix products, arithmetic and copies ran while one was open for 0% of the time, Pallas kernels for 0%

commit v1 on v0

v1 whole, which is shorter than its diff:
```python
import functools
import math

import jax
import jax.numpy as jnp
import numpy as np
from jax import lax
from jax.experimental import pallas as pl
from jax.experimental.pallas import tpu as pltpu
from jax.sharding import PartitionSpec as P

NORM_EPS = 1e-6
ROPE_THETA = 10000.0
MASKED = -1e30
FLOOR = -1e29
F32, BF16 = jnp.float32, jnp.bfloat16
MESH = pl.DeviceIdType.MESH
NT = (((1,), (1,)), ((), ()))
LANES = 128


def dot(a, b):
    return jnp.dot(a, b, preferred_element_type=F32)


def dot_nt(a, b):
    return lax.dot_general(a, b, NT, preferred_element_type=F32)


def rounded(v):
    return v.astype(BF16).astype(F32)


def wait_bytes(view, sem):
    pltpu.make_async_copy(view, view, sem).wait()


def step_kernel(dims, x_h, wdq_h, gq_h, wuq_h, wdkv_h, gkv_h, wuk_h, wuv_h, wo_h, cc_h, kr_h, freq_h, ctx_s,
                xo_h, cn_h, krn_h,
                x_v, wdq_v, gq_v, wuq_v, wdkv_v, gkv_v, wuk_v, wuv_v, wo_v, cc_v, kr_v, freq_v, wv_v,
                xf_v, cqp_v, kvp_v, qn_v, q_v, cnf_v, acc_v, pair_v, rs_v, rsr_v, olat_v, po_v, pop_v, pt_v, ptr_v, ag_v,
                xo_v, cno_v, krno_v,
                in_sem, uq_sem, uk_sem, cc_sem, out_sem,
                a_send, a_recv, kv_send, kv_recv, q_send, q_recv, pair_send, pair_recv, rs_send, rs_recv,
                po_send, po_recv, pt_send, pt_recv, ag_send, ag_recv, ag2_send, ag2_recv):
    cp, side = dims
    chips = cp // 2
    inner = 2 * side
    nreq, dmodel = x_v.shape
    kdq, ndq = wdq_v.shape
    latent, half_heads, nope = wuk_v.shape
    heads = 2 * half_heads
    rope = kr_v.shape[1]
    half_rope = rope // 2
    tdev = cc_v.shape[1]
    wide = latent + LANES
    qk = nope + rope
    kdkv = wdkv_v.shape[1]
    slab = 8
    own = heads // cp

    d = lax.axis_index('cp')
    c = lax.rem(d, 2)
    t = d // 2
    oc = 1 - c
    gi = lax.rem(d, inner)
    base = d - gi
    xx = gi // 2
    partner = base + 2 * xx + oc

    def chip_at(r):
        return lax.rem(t + r, chips)

    def local(src, dst, sem):
        cpy = pltpu.make_async_copy(src, dst, sem)
        cpy.start()
        return cpy

    cx = local(x_h, x_v, in_sem.at[0])
    cdq = local(wdq_h.at[pl.ds(pl.multiple_of(c * kdq, kdq), kdq), pl.ds(pl.multiple_of(xx * ndq, LANES), ndq)], wdq_v, in_sem.at[1])
    cdkv = local(wdkv_h.at[:, pl.ds(pl.multiple_of(gi * kdkv, LANES), kdkv)], wdkv_v, in_sem.at[2])
    cgq = local(gq_h, gq_v, in_sem.at[3])
    cgkv = local(gkv_h, gkv_v, in_sem.at[4])
    cfreq = local(freq_h, freq_v, in_sem.at[5])
    nslab = half_heads // slab
    uk = [local(wuk_h.at[:, pl.ds(pl.multiple_of(c * half_heads + s * slab, slab), slab), :],
                wuk_v.at[:, pl.ds(s * slab, slab), :], uk_sem.at[s]) for s in range(nslab)]
    nuq = wuq_v.shape[1] // 768
    uq = [local(wuq_h.at[:, pl.ds(pl.multiple_of(c * nuq * 768 + j * 768, LANES), 768)],
                wuq_v.at[:, pl.ds(j * 768, 768)], uq_sem.at[j]) for j in range(nuq)]
    for b in range(nreq):
        local(cc_h.at[b], cc_v.at[b], cc_sem.at[0, b])
        local(kr_h.at[b], kr_v.at[b], cc_sem.at[1, b])
    head0 = c * half_heads + t * own
    head_slab = head0 // slab
    head_in = head0 - head_slab * slab
    cuv = local(wuv_h.at[:, pl.ds(pl.multiple_of(head_slab * slab, slab), slab), :], wuv_v, in_sem.at[6])
    cwo = local(wo_h.at[pl.ds(pl.multiple_of(head0 * nope, own * nope), own * nope), :], wo_v, in_sem.at[7])

    barrier = pltpu.get_barrier_semaphore()

    def greet(r, _):
        pl.semaphore_signal(barrier, inc=1, device_id={'cp': 2 * chip_at(r) + c}, device_id_type=MESH)
        return 0

    lax.fori_loop(1, chips, greet, 0)
    for i in range(side):
        pl.semaphore_signal(barrier, inc=1, device_id={'cp': base + 2 * i + oc}, device_id_type=MESH)

    cx.wait()
    cdq.wait()
    part = dot(x_v[:, pl.ds(pl.multiple_of(c * kdq, kdq), kdq)], wdq_v[...])
    cqp_v[gi] = part
    pl.semaphore_wait(barrier, chips - 1 + side)

    def to_ring(buf, send, recv):
        def go(r, _):
            peer = lax.rem(gi + r, inner)
            pltpu.make_async_remote_copy(src_ref=buf.at[gi], dst_ref=buf.at[gi], send_sem=send, recv_sem=recv,
                                         device_id={'cp': base + peer}, device_id_type=MESH).start()
            return 0
        lax.fori_loop(1, inner, go, 0)

    to_ring(cqp_v, a_send, a_recv)
    cdkv.wait()
    kvp_v[gi, :, 0:latent + rope] = dot_nt(x_v[:, pl.ds(pl.multiple_of(gi * kdkv, LANES), kdkv)], wdkv_v[...])
    kvp_v[gi, :, latent + rope:] = jnp.zeros((nreq, wide - latent - rope), F32)
    to_ring(kvp_v, kv_send, kv_recv)

    xall = x_v[...].astype(F32)
    for i in range(2):
        xf_v[i] = xall[4 * i:4 * i + 4, :]
    rows = lax.broadcasted_iota(jnp.int32, (nreq, LANES), 0)
    ctx = jnp.zeros((nreq, LANES), jnp.int32)
    for b in range(nreq):
        ctx = jnp.where(rows == b, ctx_s[b], ctx)
    cfreq.wait()
    angles = ctx.astype(F32) * freq_v[...]
    cos_full = jnp.cos(angles)[:, :rope]
    sin_raw = jnp.sin(angles)[:, :rope]
    lane = lax.broadcasted_iota(jnp.int32, (nreq, rope), 1)
    sin_full = jnp.where(lane < half_rope, -sin_raw, sin_raw)

    def rope_rotate(v):
        swapped = jnp.concatenate([v[:, half_rope:], v[:, :half_rope]], axis=1)
        return v * cos_full + swapped * sin_full

    wait_bytes(cqp_v.at[pl.ds(0, inner - 1)], a_recv)
    cols = [cqp_v[2 * i] + cqp_v[2 * i + 1] for i in range(side)]
    cq = rounded(jnp.concatenate(cols, axis=1))
    cgq.wait()
    mean_sq = jnp.mean(cq * cq, axis=1, keepdims=True)
    cn = (cq * lax.rsqrt(mean_sq + NORM_EPS) * gq_v[...]).astype(BF16)
    row0 = c * half_heads * nreq
    zeros_pad = jnp.zeros((nreq, LANES - rope), F32)
    for j in range(nuq):
        uq[j].wait()
        qc = rounded(dot(cn, wuq_v[:, j * 768:(j + 1) * 768]))
        for i in range(768 // qk):
            h = j * (768 // qk) + i
            qn_v[h * nreq:(h + 1) * nreq, :] = qc[:, i * qk:i * qk + nope]
            qr = rounded(rope_rotate(qc[:, i * qk + nope:(i + 1) * qk]))
            r = pl.multiple_of(row0 + h * nreq, nreq)
            q_v[latent // LANES, pl.ds(r, nreq), :] = jnp.concatenate([qr, zeros_pad], axis=1)

    def q_slab_copy(s):
        view = q_v.at[:, pl.ds(pl.multiple_of(row0 + s * slab * nreq, slab * nreq), slab * nreq)]
        return pltpu.make_async_remote_copy(src_ref=view, dst_ref=view, send_sem=q_send.at[s], recv_sem=q_recv.at[s],
                                            device_id={'cp': partner}, device_id_type=MESH)

    for s in range(nslab):
        uk[s].wait()
        for i in range(slab):
            h = s * slab + i
            ql = rounded(dot_nt(qn_v[h * nreq:(h + 1) * nreq, :].astype(BF16), wuk_v[:, h, :]))
            r = pl.multiple_of(row0 + h * nreq, nreq)
            for k in range(latent // LANES):
                q_v[k, pl.ds(r, nreq), :] = ql[:, k * LANES:(k + 1) * LANES]
        q_slab_copy(s).start()

    wait_bytes(kvp_v.at[pl.ds(0, inner - 1)], kv_recv)
    kv = kvp_v[0]
    for i in range(1, inner):
        kv = kv + kvp_v[i]
    kvl = kv[:, :latent]
    cgkv.wait()
    mean_sq = jnp.mean(kvl * kvl, axis=1, keepdims=True)
    c_new = kvl * lax.rsqrt(mean_sq + NORM_EPS) * gkv_v[...]
    kr_new = rope_rotate(kv[:, latent:latent + rope])
    cno_v[...] = c_new.astype(BF16)
    krno_v[...] = kr_new.astype(BF16)
    cnf_v[:, :latent] = rounded(c_new)
    cnf_v[:, latent:] = jnp.concatenate([rounded(kr_new), zeros_pad], axis=1)
    ocn = local(cno_v, cn_h, out_sem.at[0])
    okr = local(krno_v, krn_h, out_sem.at[1])

    for s in range(nslab):
        q_slab_copy(s).wait()

    scale = (nope + rope) ** -0.5
    block0 = d * tdev
    key_pos = lax.broadcasted_iota(jnp.int32, (heads, tdev), 1)
    head_row = lax.broadcasted_iota(jnp.int32, (heads, 1), 0)
    lane1 = lax.broadcasted_iota(jnp.int32, (half_heads, LANES), 1)
    mine0 = pl.multiple_of(c * half_heads, half_heads)
    theirs0 = pl.multiple_of(oc * half_heads, half_heads)

    def pair_copy(b):
        return pltpu.make_async_remote_copy(src_ref=acc_v.at[b, pl.ds(theirs0, half_heads)], dst_ref=pair_v.at[b],
                                            send_sem=pair_send.at[b], recv_sem=pair_recv.at[b],
                                            device_id={'cp': partner}, device_id_type=MESH)

    def attend(b):
        pltpu.make_async_copy(cc_v.at[b], cc_v.at[b], cc_sem.at[0, b]).wait()
        pltpu.make_async_copy(kr_v.at[b], kr_v.at[b], cc_sem.at[1, b]).wait()
        qf = jnp.concatenate([q_v[k, pl.ds(b, heads, stride=nreq), :] for k in range(wide // LANES)], axis=1)
        qb = qf.astype(BF16)
        s = (dot_nt(qb[:, :latent], cc_v[b]) + dot(qb[:, latent:latent + rope], kr_v[b])) * scale
        left = ctx_s[b] - block0
        s = jnp.where(key_pos < left, s, MASKED)
        new_row = cnf_v[pl.ds(b, 1), :]
        new_s = jnp.sum(qf * new_row, axis=1, keepdims=True) * scale
        at = head_row * 0 + left
        owner = jnp.logical_and(at >= 0, at < tdev)
        new_s = jnp.where(owner, new_s, MASKED)
        m = jnp.maximum(jnp.maximum(jnp.max(s, axis=1, keepdims=True), new_s), FLOOR)
        p = jnp.exp(s - m)
        new_w = jnp.exp(new_s - m)
        l = jnp.sum(p, axis=1, keepdims=True) + new_w
        acc = dot(p.astype(BF16), cc_v[b]) + rounded(new_w) * new_row[:, :latent]
        acc_v[b, :, :latent] = acc
        ml_lane = lax.broadcasted_iota(jnp.int32, (heads, LANES), 1)
        acc_v[b, :, latent:] = jnp.where(ml_lane < LANES // 2, m, l)
        pair_copy(b).start()

    def rs_copy(b, r):
        return pltpu.make_async_remote_copy(src_ref=rs_v.at[b, chip_at(r)], dst_ref=rsr_v.at[b, r - 1],
                                            send_sem=rs_send.at[b], recv_sem=rs_recv.at[b],
                                            device_id={'cp': 2 * chip_at(r) + c}, device_id_type=MESH)

    def pair_merge(b):
        pair_copy(b).wait_recv()
        a1 = acc_v[b, pl.ds(mine0, half_heads), :]
        a2 = pair_v[b]
        m1, m2 = a1[:, latent:latent + 1], a2[:, latent:latent + 1]
        l1, l2 = a1[:, wide - 1:wide], a2[:, wide - 1:wide]
        m = jnp.maximum(m1, m2)
        f1, f2 = jnp.exp(m1 - m), jnp.exp(m2 - m)
        acc = f1 * a1[:, :latent] + f2 * a2[:, :latent]
        ml = jnp.where(lane1 < LANES // 2, m, f1 * l1 + f2 * l2)
        for k in range(chips):
            rs_v[b, k, :, :latent] = acc[own * k:own * (k + 1), :]
            rs_v[b, k, :, latent:] = ml[own * k:own * (k + 1), :]

        def go(r, _):
            rs_copy(b, r).start()
            return 0
        lax.fori_loop(1, chips, go, 0)

    def attend_step(b, _):
        attend(b)

        @pl.when(b > 0)
        def _():
            pair_merge(b - 1)
        return 0

    lax.fori_loop(0, nreq, attend_step, 0)
    pair_merge(nreq - 1)

    cuv.wait()
    for i in range(slab // own):
        @pl.when(head_in == i * own)
        def _():
            for k in range(own):
                wv_v[k] = wuv_v[:, i * own + k, :]

    def owner_merge(b, _):
        wait_bytes(rsr_v.at[b], rs_recv.at[b])
        first = rs_v[b, t]
        rest = rsr_v[b]
        m0, l0 = first[:, latent:latent + 1], first[:, wide - 1:wide]
        mr, lr = rest[:, :, latent:latent + 1], rest[:, :, wide - 1:wide]
        m = jnp.maximum(jnp.max(mr, axis=0), m0)
        f0, fr = jnp.exp(m0 - m), jnp.exp(mr - m[None])
        l = f0 * l0 + jnp.sum(fr * lr, axis=0)
        acc = f0 * first[:, :latent] + jnp.sum(fr * rest[:, :, :latent], axis=0)
        ol = rounded(acc / l)
        for k in range(own):
            olat_v[k, pl.ds(b, 1), :] = ol[k:k + 1, :]
        return 0

    lax.fori_loop(0, nreq, owner_merge, 0)

    cwo.wait()
    outs = []
    for k in range(own):
        outs.append(dot(olat_v[k].astype(BF16), wv_v[k]).astype(BF16))
    o = jnp.concatenate(outs, axis=1)
    ncol = 768
    for j in range(dmodel // ncol):
        pj = dot(o, wo_v[:, j * ncol:(j + 1) * ncol])
        for i in range(2):
            po_v[i, :, j * ncol:(j + 1) * ncol] = pj[4 * i:4 * i + 4, :]
    po_copy = pltpu.make_async_remote_copy(src_ref=po_v.at[oc], dst_ref=pop_v, send_sem=po_send, recv_sem=po_recv,
                                           device_id={'cp': partner}, device_id_type=MESH)
    po_copy.start()
    po_copy.wait()
    tcol = dmodel // chips
    for k in range(chips):
        pt_v[k] = po_v[c, :, k * tcol:(k + 1) * tcol] + pop_v[:, k * tcol:(k + 1) * tcol]

    def pt_go(r, _):
        pltpu.make_async_remote_copy(src_ref=pt_v.at[chip_at(r)], dst_ref=ptr_v.at[r - 1], send_sem=pt_send, recv_sem=pt_recv,
                                     device_id={'cp': 2 * chip_at(r) + c}, device_id_type=MESH).start()
        return 0
    lax.fori_loop(1, chips, pt_go, 0)
    wait_bytes(ptr_v, pt_recv)
    tot = pt_v[t]
    for r in range(chips - 1):
        tot = tot + ptr_v[r]
    ag_v[c, t] = rounded(xf_v[c, :, pl.ds(pl.multiple_of(t * tcol, LANES), tcol)] + tot)

    def ag_go(r, _):
        pltpu.make_async_remote_copy(src_ref=ag_v.at[c, t], dst_ref=ag_v.at[c, t], send_sem=ag_send, recv_sem=ag_recv,
                                     device_id={'cp': 2 * chip_at(r) + c}, device_id_type=MESH).start()
        return 0
    lax.fori_loop(1, chips, ag_go, 0)
    wait_bytes(ag_v.at[0, pl.ds(0, chips - 1)], ag_recv)
    ag_copy = pltpu.make_async_remote_copy(src_ref=ag_v.at[c], dst_ref=ag_v.at[c], send_sem=ag2_send, recv_sem=ag2_recv,
                                           device_id={'cp': partner}, device_id_type=MESH)
    ag_copy.start()
    ag_copy.wait()
    for k in range(chips):
        xo_v[:, k * tcol:(k + 1) * tcol] = jnp.concatenate([ag_v[0, k], ag_v[1, k]], axis=0).astype(BF16)
    oxo = local(xo_v, xo_h, out_sem.at[2])

    wait_bytes(cqp_v.at[pl.ds(0, inner - 1)], a_send)
    wait_bytes(kvp_v.at[pl.ds(0, inner - 1)], kv_send)
    wait_bytes(ptr_v, pt_send)
    wait_bytes(ag_v.at[0, pl.ds(0, chips - 1)], ag_send)

    def drain(b, _):
        pair_copy(b).wait_send()
        wait_bytes(rsr_v.at[b], rs_send.at[b])
        return 0
    lax.fori_loop(0, nreq, drain, 0)
    ocn.wait()
    okr.wait()
    oxo.wait()


def solution(mesh):
    cp = mesh.shape['cp']
    side = math.isqrt(cp // 2)
    inner = 2 * side
    chips = cp // 2

    def decode_step(x, w_dq, g_q, w_uq, w_dkv, g_kv, w_uk, w_uv, w_o, cache_c, cache_kr, ctx_len):
        nreq, dmodel = x.shape
        qlora = w_dq.shape[1]
        latent, heads, nope = w_uk.shape
        rope = cache_kr.shape[2]
        tdev = cache_c.shape[1]
        half = heads // 2
        own = heads // cp
        wide = latent + LANES
        tcol = dmodel // chips
        inv = (np.float64(ROPE_THETA) ** (-2.0 * np.arange(rope // 2) / rope)).astype(np.float32)
        freq = np.zeros((1, LANES), np.float32)
        freq[0, :rope] = np.concatenate([inv, inv])
        anyspec = pl.BlockSpec(memory_space=pl.ANY)
        dma = pltpu.SemaphoreType.DMA
        vm = pltpu.VMEM
        out_shape = (jax.ShapeDtypeStruct((nreq, dmodel), BF16), jax.ShapeDtypeStruct((nreq, latent), BF16),
                     jax.ShapeDtypeStruct((nreq, rope), BF16))
        scratch = [
            vm((nreq, dmodel), BF16), vm((dmodel // 2, qlora // side), BF16), vm((1, qlora), F32),
            vm((qlora, w_uq.shape[1] // 2), BF16), vm((w_dkv.shape[1], dmodel // inner), BF16), vm((1, latent), F32),
            vm((latent, half, nope), BF16), vm((latent, 8, nope), BF16), vm((own * nope, dmodel), BF16),
            vm((nreq, tdev, latent), BF16), vm((nreq, rope, tdev), BF16), vm((1, LANES), F32), vm((own, latent, nope), BF16),
            vm((2, nreq // 2, dmodel), F32), vm((inner, nreq, qlora // side), F32), vm((inner, nreq, wide), F32),
            vm((half * nreq, nope), F32), vm((wide // LANES, heads * nreq, LANES), F32), vm((nreq, wide), F32),
            vm((nreq, heads, wide), F32), vm((nreq, half, wide), F32),
            vm((nreq, chips, own, wide), F32), vm((nreq, chips - 1, own, wide), F32), vm((own, nreq, latent), F32),
            vm((2, nreq // 2, dmodel), F32), vm((nreq // 2, dmodel), F32),
            vm((chips, nreq // 2, tcol), F32), vm((chips - 1, nreq // 2, tcol), F32), vm((2, chips, nreq // 2, tcol), F32),
            vm((nreq, dmodel), BF16), vm((nreq, latent), BF16), vm((nreq, rope), BF16),
            dma((8,)), dma((w_uq.shape[1] // 2 // 768,)), dma((half // 8,)), dma((2, nreq)), dma((3,)),
            dma, dma, dma, dma, dma((half // 8,)), dma((half // 8,)), dma((nreq,)), dma((nreq,)), dma((nreq,)), dma((nreq,)),
            dma, dma, dma, dma, dma, dma, dma, dma,
        ]
        return pl.pallas_call(
            functools.partial(step_kernel, (cp, side)),
            out_shape=out_shape,
            in_specs=[anyspec] * 12 + [pl.BlockSpec(memory_space=pltpu.SMEM)],
            out_specs=(anyspec,) * 3,
            scratch_shapes=scratch,
            compiler_params=pltpu.CompilerParams(collective_id=0, has_side_effects=True, vmem_limit_bytes=67043328),
            name='decode_step',
        )(x, w_dq, g_q.reshape(1, qlora), w_uq, w_dkv.T, g_kv.reshape(1, latent), w_uk, w_uv, w_o,
          cache_c, jnp.swapaxes(cache_kr, 1, 2), jnp.asarray(freq), ctx_len)

    spec_rows = P('dp', None)
    spec_cache = P('dp', 'cp', None)
    in_specs = (spec_rows, P(), P(), P(), P(), P(), P(), P(), P(), spec_cache, spec_cache, P('dp'))
    out_specs = (spec_rows, spec_rows, spec_rows)
    return jax.shard_map(decode_step, mesh=mesh, in_specs=in_specs, out_specs=out_specs, check_vma=False)
```

time: 372 us -> 71.5 us (0.19); the launches traced: 367 us -> 71.3 us
  waiting for transfers between devices: 134 us -> 0 us
  matrix products: 114 us -> 0 us
  local copies, waits for them, and re-layouts: 74 us -> 5.38 us
  Pallas kernels: 0 us -> 65.3 us
  other arithmetic: 29.6 us -> 0 us
  between operations: 14.7 us -> 0.64 us
    all_gather x1 -> x0, waiting for transfers between devices: 134 us -> none  [decode_step(): gathered = lax.all_gather(packed, 'cp')]
    dot_general x10 -> x0, matrix products: 114 us -> none  [the longest x1 39.1 us: output_step(): jnp.dot(o_heads.reshape(x.shape[0], -1), w_o, preferred_element_type=jnp....]
    all_gather x1 -> x0, local copies, waits for them, and re-layouts: 70.8 us -> none  [decode_step(): gathered = lax.all_gather(packed, 'cp')]
    pallas_call x0 -> x1, Pallas kernels: none -> 65.3 us  [decode_step(): pl.pallas_call(functools.partial(step_kernel, (cp, side)), out_shape=out_...]
    reduce_sum x4 -> x0, other arithmetic: 23.8 us -> none  [the longest x1 21.5 us: decode_step(): lat_sum = jnp.sum(factor[:, :, :, None] * gathered[:, :, :, 2:], axis=0)]
  transfers between devices with their start and end apart: 1 -> 0, of which waited for: 1 -> 0; matrix products, arithmetic and copies ran while one was open for 0% -> 0% of each run, Pallas kernels for 0% -> 0%
where the time goes in v1:
time: 71.5 us; the launch traced here: 71.3 us
  Pallas kernels  65.3 us (91%)
  local copies, waits for them, and re-layouts  5.38 us (8%)
    pallas_call x1, Pallas kernels, decode_step(): pl.pallas_call(functools.partial(step_kernel, (cp, side)), out_shape=out_...  65.3 us
    unnamed x3, local copies, waits for them, and re-layouts  4.08 us

profile of v1, /device:TPU:97, one launch (start us, length us, event | category | flops | bytes accessed | tf_op | source)
XLA Modules:
  0.0 71.3 jit_solution(9472314176265085915)
XLA Ops:
  0.6 1.3 %reshape.12.gq_h = f32[1,1536]{1,0:T(1,128)} reshape(f32[1536]{0:T(1024)} %param.15) | data formatting | bytes 12288 | tf_op jit(solution)/shard_map/reshape | solution.py:401
  1.9 65.3 %decode_step.1 = (bf16[8,6144]{1,0:T(8,128)(2,1)}, bf16[8,512]{1,0:T(8,128)(2,1)}, bf16[8,64]{1,0:T(8,128)(2,1)}) custom-call(bf16[8,6144]{1,0:T(8,128)(2,1)} %x_h.1, bf16[6144,1536]{1,0:T(8,128)(2,1)} %wdq_h.1, f32[1,1536]{1,0:T(1,128)} %reshape.12.gq_h, bf16[1536,12288]{1,0:T(8,128)(2,1)} %wuq_h.1, bf16[576,6144]{1,0:T(8,128)(2,1)} %bitcast.3, ...), custom_call_target="tpu_custom_call" | custom-call | tf_op jit(solution)/shard_map/decode_step/pallas_call | solution.py:393
  67.2 1.5 %copy.19 = bf16[8,6144]{1,0:T(8,128)(2,1)} copy(bf16[8,6144]{1,0:T(8,128)(2,1)} %get-tuple-element.6) | data formatting | bytes 196608
  68.7 1.3 %copy.20 = bf16[8,512]{1,0:T(8,128)(2,1)} copy(bf16[8,512]{1,0:T(8,128)(2,1)} %get-tuple-element.7) | data formatting | bytes 16384
  70.0 1.2 %copy.21 = bf16[8,64]{1,0:T(8,128)(2,1)} copy(bf16[8,64]{1,0:T(8,128)(2,1)} %get-tuple-element.8) | data formatting | bytes 2048

commit v2 on v1

v2 whole, which is shorter than its diff:
```python
import functools
import math

import jax
import jax.numpy as jnp
import numpy as np
from jax import lax
from jax.experimental import pallas as pl
from jax.experimental.pallas import tpu as pltpu
from jax.sharding import PartitionSpec as P

NORM_EPS = 1e-6
ROPE_THETA = 10000.0
MASKED = -1e30
FLOOR = -1e29
F32, BF16 = jnp.float32, jnp.bfloat16
MESH = pl.DeviceIdType.MESH
NT = (((1,), (1,)), ((), ()))
LANES = 128


def dot(a, b):
    return jnp.dot(a, b, preferred_element_type=F32)


def dot_nt(a, b):
    return lax.dot_general(a, b, NT, preferred_element_type=F32)


def rounded(v):
    return v.astype(BF16).astype(F32)


def wait_bytes(view, sem):
    pltpu.make_async_copy(view, view, sem).wait()


def step_kernel(dims, x_h, wdq_h, gq_h, wuq_h, wdkv_h, gkv_h, wuk_h, wuv_h, wo_h, cc_h, kr_h, freq_h, ctx_s,
                out_v,
                x_v, wdq_v, gq_v, wuq_v, wdkv_v, gkv_v, wuk_v, wuv_v, wo_v, cc_v, kr_v, freq_v, wv_v, wk_v, stage_v,
                xf_v, cqp_v, kvp_v, q_v, cnf_v, acc_v, pair_v, xs_v, xsr_v, ys_v, ysr_v, olat_v, po_v, pop_v, pt_v, ptr_v, ag_v,
                in_sem, uq_sem, uk_sem, cc_sem,
                a_send, a_recv, kv_send, kv_recv, q_send, q_recv, pair_send, pair_recv, xs_send, xs_recv, ys_send, ys_recv,
                po_send, po_recv, pt_send, pt_recv, ag_send, ag_recv, ag2_send, ag2_recv):
    cp, side = dims
    chips = cp // 2
    inner = 2 * side
    nreq, dmodel = x_v.shape
    kdq, ndq = wdq_v.shape
    nslab, latent, slab, nope = wuk_v.shape
    half_heads = nslab * slab
    heads = 2 * half_heads
    rope = kr_v.shape[1]
    half_rope = rope // 2
    tdev = cc_v.shape[1]
    wide = latent + LANES
    qk = nope + rope
    kdkv = wdkv_v.shape[1]
    own = heads // cp

    d = lax.axis_index('cp')
    c = lax.rem(d, 2)
    t = d // 2
    oc = 1 - c
    gi = lax.rem(d, inner)
    base = d - gi
    xx = gi // 2
    yy = d // inner
    partner = base + 2 * xx + oc

    kstep = 64

    def widen(src):
        def go(i, _):
            r = pl.multiple_of(i * kstep, kstep)
            stage_v[pl.ds(pl.multiple_of(r * slab, kstep * slab), kstep * slab), :] = (
                src[pl.ds(r, kstep)].astype(F32).reshape(kstep * slab, nope))
            return 0
        lax.fori_loop(0, latent // kstep, go, 0)

    def chip_at(r):
        return lax.rem(t + r, chips)

    pending = {}

    def done(name):
        pending.pop(name)()

    def drain():
        for name in list(pending):
            done(name)

    def local(name, src, dst, sem):
        cpy = pltpu.make_async_copy(src, dst, sem)
        cpy.start()
        pending[name] = cpy.wait

    later = []

    def issue(n):
        for _ in range(min(n, len(later))):
            for args in later.pop(0):
                local(*args)

    local('x', x_h, x_v, in_sem.at[0])
    local('dq', wdq_h.at[pl.ds(pl.multiple_of(c * kdq, kdq), kdq), pl.ds(pl.multiple_of(xx * ndq, LANES), ndq)], wdq_v, in_sem.at[1])
    local('dkv', wdkv_h.at[:, pl.ds(pl.multiple_of(gi * kdkv, LANES), kdkv)], wdkv_v, in_sem.at[2])
    local('gq', gq_h, gq_v, in_sem.at[3])
    local('gkv', gkv_h, gkv_v, in_sem.at[4])
    local('freq', freq_h, freq_v, in_sem.at[5])
    ucol = 768
    nuq = wuq_v.shape[1] // ucol
    for s in range(nslab):
        local(('uk', s), wuk_h.at[:, pl.ds(pl.multiple_of(c * half_heads + s * slab, slab), slab), :], wuk_v.at[s], uk_sem.at[s])
    for j in range(nuq):
        later.append([(('uq', j), wuq_h.at[:, pl.ds(pl.multiple_of(c * nuq * ucol + j * ucol, LANES), ucol)],
                       wuq_v.at[:, pl.ds(j * ucol, ucol)], uq_sem.at[j])])
    for b in range(nreq):
        later.append([(('cc', b), cc_h.at[b], cc_v.at[b], cc_sem.at[0, b]), (('kr', b), kr_h.at[b], kr_v.at[b], cc_sem.at[1, b])])
    head0 = c * half_heads + xx * slab + yy * own
    head_slab = head0 // slab
    head_in = head0 - head_slab * slab
    later.append([('uv', wuv_h.at[:, pl.ds(pl.multiple_of(head_slab * slab, slab), slab), :], wuv_v, in_sem.at[6])])
    later.append([('wo', wo_h.at[pl.ds(pl.multiple_of(head0 * nope, own * nope), own * nope), :], wo_v, in_sem.at[7])])

    barrier = pltpu.get_barrier_semaphore()

    def greet(r, _):
        pl.semaphore_signal(barrier, inc=1, device_id={'cp': 2 * chip_at(r) + c}, device_id_type=MESH)
        return 0

    lax.fori_loop(1, chips, greet, 0)
    for i in range(side):
        pl.semaphore_signal(barrier, inc=1, device_id={'cp': base + 2 * i + oc}, device_id_type=MESH)

    done('x')
    done('dq')
    part = dot(x_v[:, pl.ds(pl.multiple_of(c * kdq, kdq), kdq)], wdq_v[...])
    cqp_v[gi] = part
    issue(2)
    pl.semaphore_wait(barrier, chips - 1 + side)

    def to_ring(buf, send, recv):
        def go(r, _):
            peer = lax.rem(gi + r, inner)
            pltpu.make_async_remote_copy(src_ref=buf.at[gi], dst_ref=buf.at[gi], send_sem=send, recv_sem=recv,
                                         device_id={'cp': base + peer}, device_id_type=MESH).start()
            return 0
        lax.fori_loop(1, inner, go, 0)

    to_ring(cqp_v, a_send, a_recv)
    issue(1)
    pending['a_send'] = lambda: wait_bytes(cqp_v.at[pl.ds(0, inner - 1)], a_send)
    pending['a_recv'] = lambda: wait_bytes(cqp_v.at[pl.ds(0, inner - 1)], a_recv)
    done('dkv')
    kvp_v[gi, :, 0:latent + rope] = dot_nt(x_v[:, pl.ds(pl.multiple_of(gi * kdkv, LANES), kdkv)], wdkv_v[...])
    kvp_v[gi, :, latent + rope:] = jnp.zeros((nreq, wide - latent - rope), F32)
    to_ring(kvp_v, kv_send, kv_recv)
    pending['kv_send'] = lambda: wait_bytes(kvp_v.at[pl.ds(0, inner - 1)], kv_send)
    pending['kv_recv'] = lambda: wait_bytes(kvp_v.at[pl.ds(0, inner - 1)], kv_recv)

    issue(1)

    xall = x_v[...].astype(F32)
    for i in range(2):
        xf_v[i] = xall[4 * i:4 * i + 4, :]
    rows = lax.broadcasted_iota(jnp.int32, (nreq, LANES), 0)
    ctx = jnp.zeros((nreq, LANES), jnp.int32)
    for b in range(nreq):
        ctx = jnp.where(rows == b, ctx_s[b], ctx)
    done('freq')
    angles = ctx.astype(F32) * freq_v[...]
    cos_full = jnp.cos(angles)[:, :rope]
    sin_raw = jnp.sin(angles)[:, :rope]
    lane = lax.broadcasted_iota(jnp.int32, (nreq, rope), 1)
    sin_full = jnp.where(lane < half_rope, -sin_raw, sin_raw)

    def rope_rotate(v):
        swapped = jnp.concatenate([v[:, half_rope:], v[:, :half_rope]], axis=1)
        return v * cos_full + swapped * sin_full

    for s in range(nslab):
        done(('uk', s))
        issue(1)
        widen(wuk_v.at[s])
        for i in range(slab):
            wk_v[s * slab + i] = stage_v[pl.ds(i, latent, stride=slab), :].astype(BF16)

    done('a_recv')
    cols = [cqp_v[2 * i] + cqp_v[2 * i + 1] for i in range(side)]
    cq = rounded(jnp.concatenate(cols, axis=1))
    done('gq')
    mean_sq = jnp.mean(cq * cq, axis=1, keepdims=True)
    cn = (cq * lax.rsqrt(mean_sq + NORM_EPS) * gq_v[...].reshape(1, gq_v.shape[0])).astype(BF16)
    row0 = c * half_heads * nreq
    zeros_pad = jnp.zeros((nreq, LANES - rope), F32)
    per = ucol // qk

    def q_slab_copy(s):
        view = q_v.at[:, pl.ds(pl.multiple_of(row0 + s * slab * nreq, slab * nreq), slab * nreq)]
        return pltpu.make_async_remote_copy(src_ref=view, dst_ref=view, send_sem=q_send.at[s], recv_sem=q_recv.at[s],
                                            device_id={'cp': partner}, device_id_type=MESH)

    for j in range(nuq):
        done(('uq', j))
        issue(1)
        qc = rounded(dot(cn, wuq_v[:, j * ucol:(j + 1) * ucol]))
        for i in range(per):
            h = j * per + i
            r = pl.multiple_of(row0 + h * nreq, nreq)
            qr = rounded(rope_rotate(qc[:, i * qk + nope:(i + 1) * qk]))
            q_v[latent // LANES, pl.ds(r, nreq), :] = jnp.concatenate([qr, zeros_pad], axis=1)
            ql = rounded(dot_nt(qc[:, i * qk:i * qk + nope].astype(BF16), wk_v[h]))
            for k in range(latent // LANES):
                q_v[k, pl.ds(r, nreq), :] = ql[:, k * LANES:(k + 1) * LANES]
        if (j + 1) * per % slab == 0:
            s = (j + 1) * per // slab - 1
            q_slab_copy(s).start()
            pending['q', s] = q_slab_copy(s).wait

    issue(len(later))

    done('kv_recv')
    kv = kvp_v[0]
    for i in range(1, inner):
        kv = kv + kvp_v[i]
    kvl = kv[:, :latent]
    done('gkv')
    mean_sq = jnp.mean(kvl * kvl, axis=1, keepdims=True)
    c_new = kvl * lax.rsqrt(mean_sq + NORM_EPS) * gkv_v[...]
    kr_new = rope_rotate(kv[:, latent:latent + rope])
    out_v[:, dmodel:dmodel + latent] = c_new.astype(BF16)
    out_v[:, dmodel + latent:] = jnp.concatenate([kr_new, zeros_pad], axis=1).astype(BF16)
    cnf_v[:, :latent] = rounded(c_new)
    cnf_v[:, latent:] = jnp.concatenate([rounded(kr_new), zeros_pad], axis=1)

    for s in range(nslab):
        done(('q', s))

    scale = (nope + rope) ** -0.5
    block0 = d * tdev
    key_pos = lax.broadcasted_iota(jnp.int32, (heads, tdev), 1)
    head_row = lax.broadcasted_iota(jnp.int32, (heads, 1), 0)
    mine0 = pl.multiple_of(c * half_heads, half_heads)
    theirs0 = pl.multiple_of(oc * half_heads, half_heads)

    def pair_copy(b):
        return pltpu.make_async_remote_copy(src_ref=acc_v.at[b, pl.ds(theirs0, half_heads)], dst_ref=pair_v.at[b],
                                            send_sem=pair_send.at[b], recv_sem=pair_recv.at[b],
                                            device_id={'cp': partner}, device_id_type=MESH)

    def attend(b):
        pltpu.make_async_copy(cc_v.at[b], cc_v.at[b], cc_sem.at[0, b]).wait()
        pltpu.make_async_copy(kr_v.at[b], kr_v.at[b], cc_sem.at[1, b]).wait()
        qf = jnp.concatenate([q_v[k, pl.ds(b, heads, stride=nreq), :] for k in range(wide // LANES)], axis=1)
        qb = qf.astype(BF16)
        s = (dot_nt(qb[:, :latent], cc_v[b]) + dot(qb[:, latent:latent + rope], kr_v[b])) * scale
        left = ctx_s[b] - block0
        s = jnp.where(key_pos < left, s, MASKED)
        new_row = cnf_v[pl.ds(b, 1), :]
        new_s = jnp.sum(qf * new_row, axis=1, keepdims=True) * scale
        at = head_row * 0 + left
        owner = jnp.logical_and(at >= 0, at < tdev)
        new_s = jnp.where(owner, new_s, MASKED)
        m = jnp.maximum(jnp.maximum(jnp.max(s, axis=1, keepdims=True), new_s), FLOOR)
        p = jnp.exp(s - m)
        new_w = jnp.exp(new_s - m)
        l = jnp.sum(p, axis=1, keepdims=True) + new_w
        acc = dot(p.astype(BF16), cc_v[b]) + rounded(new_w) * new_row[:, :latent]
        acc_v[b, :, :latent] = acc
        ml_lane = lax.broadcasted_iota(jnp.int32, (heads, LANES), 1)
        acc_v[b, :, latent:] = jnp.where(ml_lane < LANES // 2, m, l)
        pair_copy(b).start()

    quarter = half_heads // side

    def xs_copy(b, r):
        px = lax.rem(xx + r, side)
        return pltpu.make_async_remote_copy(src_ref=xs_v.at[b, pl.ds(pl.multiple_of(px * quarter, quarter), quarter)],
                                            dst_ref=xsr_v.at[b, r - 1], send_sem=xs_send.at[b], recv_sem=xs_recv.at[b],
                                            device_id={'cp': base + 2 * px + c}, device_id_type=MESH)

    def ys_copy(b, r):
        py = lax.rem(yy + r, side)
        return pltpu.make_async_remote_copy(src_ref=ys_v.at[b, py], dst_ref=ysr_v.at[b, r - 1],
                                            send_sem=ys_send.at[b], recv_sem=ys_recv.at[b],
                                            device_id={'cp': py * inner + gi}, device_id_type=MESH)

    def ml_of(v):
        return v[:, latent:latent + 1], v[:, wide - 1:wide]

    def merge(parts):
        ms, ls = zip(*[ml_of(p) for p in parts])
        m = functools.reduce(jnp.maximum, ms)
        fs = [jnp.exp(mi - m) for mi in ms]
        l = sum(f * li for f, li in zip(fs, ls))
        acc = sum(f * p[:, :latent] for f, p in zip(fs, parts))
        return m, l, acc

    def with_ml(m, l):
        side_lane = lax.broadcasted_iota(jnp.int32, (m.shape[0], LANES), 1)
        return jnp.where(side_lane < LANES // 2, m, l)

    def pair_merge(b):
        pair_copy(b).wait_recv()
        m, l, acc = merge([acc_v[b, pl.ds(mine0, half_heads), :], pair_v[b]])
        xs_v[b, :, :latent] = acc
        xs_v[b, :, latent:] = with_ml(m, l)
        for r in range(1, side):
            xs_copy(b, r).start()

    def ring_merge(b):
        wait_bytes(xsr_v.at[b], xs_recv.at[b])
        mine = xs_v[b, pl.ds(pl.multiple_of(xx * quarter, quarter), quarter), :]
        m, l, acc = merge([mine] + [xsr_v[b, r] for r in range(side - 1)])
        ml = with_ml(m, l)
        for k in range(side):
            ys_v[b, k, :, :latent] = acc[own * k:own * (k + 1), :]
            ys_v[b, k, :, latent:] = ml[own * k:own * (k + 1), :]
        for r in range(1, side):
            ys_copy(b, r).start()

    lag = 4

    def attend_step(b, _):
        attend(b)

        @pl.when(b > 0)
        def _():
            pair_merge(b - 1)

        @pl.when(b >= lag)
        def _():
            ring_merge(b - lag)
        return 0

    lax.fori_loop(0, nreq, attend_step, 0)
    for b in range(nreq):
        pending.pop(('cc', b))
        pending.pop(('kr', b))
        pending['pair', b] = pair_copy(b).wait_send
    pair_merge(nreq - 1)

    def ring_step(b, _):
        ring_merge(b)
        return 0

    lax.fori_loop(nreq - lag, nreq, ring_step, 0)

    def each(view, sem):
        def go(b, _):
            wait_bytes(view.at[b], sem.at[b])
            return 0
        return lambda: lax.fori_loop(0, nreq, go, 0)

    pending['xs_send'] = each(xsr_v, xs_send)
    pending['ys_send'] = each(ysr_v, ys_send)
    pending['ys_recv'] = each(ysr_v, ys_recv)

    done('uv')
    widen(wuv_v)
    for k in range(own):
        wv_v[k] = stage_v[pl.ds(head_in + k, latent, stride=slab), :].astype(BF16)

    def owner_merge(b, _):
        wait_bytes(ysr_v.at[b], ys_recv.at[b])
        m, l, acc = merge([ys_v[b, yy]] + [ysr_v[b, r] for r in range(side - 1)])
        ol = rounded(acc / l)
        for k in range(own):
            olat_v[k, pl.ds(b, 1), :] = ol[k:k + 1, :]
        return 0

    lax.fori_loop(0, nreq, owner_merge, 0)
    pending.pop('ys_recv')

    done('wo')
    outs = []
    for k in range(own):
        outs.append(dot(olat_v[k].astype(BF16), wv_v[k]).astype(BF16))
    o = jnp.concatenate(outs, axis=1)
    ncol = 768
    for j in range(dmodel // ncol):
        pj = dot(o, wo_v[:, j * ncol:(j + 1) * ncol])
        for i in range(2):
            po_v[i, :, j * ncol:(j + 1) * ncol] = pj[4 * i:4 * i + 4, :]
    po_copy = pltpu.make_async_remote_copy(src_ref=po_v.at[oc], dst_ref=pop_v, send_sem=po_send, recv_sem=po_recv,
                                           device_id={'cp': partner}, device_id_type=MESH)
    po_copy.start()
    po_copy.wait()
    tcol = dmodel // chips
    for k in range(chips):
        pt_v[k] = po_v[c, :, k * tcol:(k + 1) * tcol] + pop_v[:, k * tcol:(k + 1) * tcol]

    def pt_go(r, _):
        pltpu.make_async_remote_copy(src_ref=pt_v.at[chip_at(r)], dst_ref=ptr_v.at[r - 1], send_sem=pt_send, recv_sem=pt_recv,
                                     device_id={'cp': 2 * chip_at(r) + c}, device_id_type=MESH).start()
        return 0
    lax.fori_loop(1, chips, pt_go, 0)
    pending['pt_send'] = lambda: wait_bytes(ptr_v, pt_send)
    wait_bytes(ptr_v, pt_recv)
    tot = pt_v[t]
    for r in range(chips - 1):
        tot = tot + ptr_v[r]
    ag_v[c, t] = rounded(xf_v[c, :, pl.ds(pl.multiple_of(t * tcol, LANES), tcol)] + tot)

    def ag_go(r, _):
        pltpu.make_async_remote_copy(src_ref=ag_v.at[c, t], dst_ref=ag_v.at[c, t], send_sem=ag_send, recv_sem=ag_recv,
                                     device_id={'cp': 2 * chip_at(r) + c}, device_id_type=MESH).start()
        return 0
    lax.fori_loop(1, chips, ag_go, 0)
    pending['ag_send'] = lambda: wait_bytes(ag_v.at[0, pl.ds(0, chips - 1)], ag_send)
    wait_bytes(ag_v.at[0, pl.ds(0, chips - 1)], ag_recv)
    ag_copy = pltpu.make_async_remote_copy(src_ref=ag_v.at[c], dst_ref=ag_v.at[c], send_sem=ag2_send, recv_sem=ag2_recv,
                                           device_id={'cp': partner}, device_id_type=MESH)
    ag_copy.start()
    ag_copy.wait()
    for k in range(chips):
        out_v[:, k * tcol:(k + 1) * tcol] = jnp.concatenate([ag_v[0, k], ag_v[1, k]], axis=0).astype(BF16)

    drain()


def split_outputs(packed_v, xo_v, cn_v, kr_v):
    dmodel, latent, rope = xo_v.shape[1], cn_v.shape[1], kr_v.shape[1]
    xo_v[...] = packed_v[:, :dmodel]
    cn_v[...] = packed_v[:, dmodel:dmodel + latent]
    kr_v[...] = packed_v[:, dmodel + latent:dmodel + latent + rope]


def solution(mesh):
    cp = mesh.shape['cp']
    side = math.isqrt(cp // 2)
    inner = 2 * side
    chips = cp // 2

    def decode_step(x, w_dq, g_q, w_uq, w_dkv, g_kv, w_uk, w_uv, w_o, cache_c, cache_kr, ctx_len):
        nreq, dmodel = x.shape
        qlora = w_dq.shape[1]
        latent, heads, nope = w_uk.shape
        rope = cache_kr.shape[2]
        tdev = cache_c.shape[1]
        half = heads // 2
        own = heads // cp
        wide = latent + LANES
        tcol = dmodel // chips
        inv = (np.float64(ROPE_THETA) ** (-2.0 * np.arange(rope // 2) / rope)).astype(np.float32)
        freq = np.zeros((1, LANES), np.float32)
        freq[0, :rope] = np.concatenate([inv, inv])
        anyspec = pl.BlockSpec(memory_space=pl.ANY)
        dma = pltpu.SemaphoreType.DMA
        vm = pltpu.VMEM
        out_shape = (jax.ShapeDtypeStruct((nreq, dmodel), BF16), jax.ShapeDtypeStruct((nreq, latent), BF16),
                     jax.ShapeDtypeStruct((nreq, rope), BF16))
        scratch = [
            vm((nreq, dmodel), BF16), vm((dmodel // 2, qlora // side), BF16), vm((qlora,), F32),
            vm((qlora, w_uq.shape[1] // 2), BF16), vm((w_dkv.shape[1], dmodel // inner), BF16), vm((1, latent), F32),
            vm((half // 8, latent, 8, nope), BF16), vm((latent, 8, nope), BF16), vm((own * nope, dmodel), BF16),
            vm((nreq, tdev, latent), BF16), vm((nreq, rope, tdev), BF16), vm((1, LANES), F32), vm((own, latent, nope), BF16),
            vm((half, latent, nope), BF16), vm((latent * 8, nope), F32),
            vm((2, nreq // 2, dmodel), F32), vm((inner, nreq, qlora // side), F32), vm((inner, nreq, wide), F32),
            vm((wide // LANES, heads * nreq, LANES), F32), vm((nreq, wide), F32),
            vm((nreq, heads, wide), F32), vm((nreq, half, wide), F32),
            vm((nreq, half, wide), F32), vm((nreq, side - 1, half // side, wide), F32),
            vm((nreq, side, own, wide), F32), vm((nreq, side - 1, own, wide), F32), vm((own, nreq, latent), F32),
            vm((2, nreq // 2, dmodel), F32), vm((nreq // 2, dmodel), F32),
            vm((chips, nreq // 2, tcol), F32), vm((chips - 1, nreq // 2, tcol), F32), vm((2, chips, nreq // 2, tcol), F32),
            dma((8,)), dma((w_uq.shape[1] // 2 // 768,)), dma((half // 8,)), dma((2, nreq)),
            dma, dma, dma, dma, dma((half // 8,)), dma((half // 8,)), dma((nreq,)), dma((nreq,)), dma((nreq,)), dma((nreq,)), dma((nreq,)), dma((nreq,)),
            dma, dma, dma, dma, dma, dma, dma, dma,
        ]
        packed = pl.pallas_call(
            functools.partial(step_kernel, (cp, side)),
            out_shape=jax.ShapeDtypeStruct((nreq, dmodel + wide), BF16),
            in_specs=[anyspec] * 12 + [pl.BlockSpec(memory_space=pltpu.SMEM)],
            out_specs=pl.BlockSpec(memory_space=pltpu.VMEM),
            scratch_shapes=scratch,
            compiler_params=pltpu.CompilerParams(collective_id=0, has_side_effects=True, vmem_limit_bytes=67043328),
            name='decode_step',
        )(x, w_dq, g_q, w_uq, w_dkv.T, g_kv.reshape(1, latent), w_uk, w_uv, w_o,
          cache_c, jnp.swapaxes(cache_kr, 1, 2), jnp.asarray(freq), ctx_len)
        vspec = pl.BlockSpec(memory_space=pltpu.VMEM)
        return pl.pallas_call(split_outputs, out_shape=out_shape, in_specs=[vspec], out_specs=(vspec,) * 3,
                              name='split_outputs')(packed)

    spec_rows = P('dp', None)
    spec_cache = P('dp', 'cp', None)
    in_specs = (spec_rows, P(), P(), P(), P(), P(), P(), P(), P(), spec_cache, spec_cache, P('dp'))
    out_specs = (spec_rows, spec_rows, spec_rows)
    return jax.shard_map(decode_step, mesh=mesh, in_specs=in_specs, out_specs=out_specs, check_vma=False)
```

time: 71.5 us -> 58.4 us (0.82)
  Pallas kernels: 65.3 us -> 57.6 us
  local copies, waits for them, and re-layouts: 5.38 us -> 0 us
    pallas_call x1 -> x2, Pallas kernels: 65.3 us -> 57.6 us  [the longest x1 56.1 us: decode_step(): pl.pallas_call(functools.partial(step_kernel, (cp, side)), out_shape=jax....]
    unnamed x3 -> x0, local copies, waits for them, and re-layouts: 4.08 us -> none
    reshape x1 -> x0, local copies, waits for them, and re-layouts: 1.3 us -> none  [decode_step(): g_q.reshape(1, qlora)]
where the time goes in v2:
time: 58.4 us; the launch traced here: 58.3 us
  Pallas kernels  57.6 us (99%)
  between operations  0.64 us (1%)
    pallas_call x1, Pallas kernels, decode_step(): pl.pallas_call(functools.partial(step_kernel, (cp, side)), out_shape=jax....  56.1 us
    pallas_call x1, Pallas kernels, decode_step(): pl.pallas_call(split_outputs, out_shape=out_shape, in_specs=[vspec], out_...  1.55 us

profile of v2, /device:TPU:97, one launch (start us, length us, event | category | flops | bytes accessed | tf_op | source)
XLA Modules:
  0.0 58.3 jit_solution(10009214370887445922)
XLA Ops:
  0.6 56.1 %decode_step.1.packed_v = bf16[8,6784]{1,0:T(8,128)(2,1)} custom-call(bf16[8,6144]{1,0:T(8,128)(2,1)} %x_h.1, bf16[6144,1536]{1,0:T(8,128)(2,1)} %wdq_h.1, f32[1536]{0:T(1024)} %gq_h.1, bf16[1536,12288]{1,0:T(8,128)(2,1)} %wuq_h.1, bf16[576,6144]{1,0:T(8,128)(2,1)} %bitcast.3, f32[1,512]{1,0:T(1,128)} %bitcast.5, bf16[512,64,128]{2,1,0:T(8,128)(2,1)} %wuk_h.1, ...), custom_call_target="tpu_custom_call" | custom-call | tf_op jit(solution)/shard_map/decode_step/pallas_call | solution.py:471
  56.7 1.5 %split_outputs.1 = (bf16[8,6144]{1,0:T(8,128)(2,1)}, bf16[8,512]{1,0:T(8,128)(2,1)}, bf16[8,64]{1,0:T(8,128)(2,1)}) custom-call(bf16[8,6784]{1,0:T(8,128)(2,1)} %decode_step.1.packed_v), custom_call_target="tpu_custom_call" | custom-call | tf_op jit(solution)/shard_map/split_outputs/pallas_call | solution.py:482

commit v3 on v2

--- a/solution.py
+++ b/solution.py
@@ -37,16 +37,15 @@
 
 def step_kernel(dims, x_h, wdq_h, gq_h, wuq_h, wdkv_h, gkv_h, wuk_h, wuv_h, wo_h, cc_h, kr_h, freq_h, ctx_s,
                 out_v,
-                x_v, wdq_v, gq_v, wuq_v, wdkv_v, gkv_v, wuk_v, wuv_v, wo_v, cc_v, kr_v, freq_v, wv_v, wk_v, stage_v,
-                xf_v, cqp_v, kvp_v, q_v, cnf_v, acc_v, pair_v, xs_v, xsr_v, ys_v, ysr_v, olat_v, po_v, pop_v, pt_v, ptr_v, ag_v,
-                in_sem, uq_sem, uk_sem, cc_sem,
+                x_v, gq_v, wuq_v, wdkv_v, gkv_v, wuk_v, wuv_v, wo_v, cc_v, kr_v, freq_v, wv_v, wk_v, stage_v,
+                xf_v, cq_v, kvp_v, q_v, cnf_v, sa_v, sb_v, m_v, acc_v, pair_v, xs_v, xsr_v, ys_v, ysr_v, olat_v, po_v, pop_v, pt_v, ptr_v, ag_v,
+                in_sem, dq_sem, uq_sem, uk_sem, cc_sem,
                 a_send, a_recv, kv_send, kv_recv, q_send, q_recv, pair_send, pair_recv, xs_send, xs_recv, ys_send, ys_recv,
                 po_send, po_recv, pt_send, pt_recv, ag_send, ag_recv, ag2_send, ag2_recv):
     cp, side = dims
     chips = cp // 2
     inner = 2 * side
     nreq, dmodel = x_v.shape
-    kdq, ndq = wdq_v.shape
     nslab, latent, slab, nope = wuk_v.shape
     half_heads = nslab * slab
     heads = 2 * half_heads
@@ -103,18 +102,22 @@
                 local(*args)
 
     local('x', x_h, x_v, in_sem.at[0])
-    local('dq', wdq_h.at[pl.ds(pl.multiple_of(c * kdq, kdq), kdq), pl.ds(pl.multiple_of(xx * ndq, LANES), ndq)], wdq_v, in_sem.at[1])
-    local('dkv', wdkv_h.at[:, pl.ds(pl.multiple_of(gi * kdkv, LANES), kdkv)], wdkv_v, in_sem.at[2])
+    nslot, krow, ucol = wuq_v.shape
+    ndq = dmodel // krow
+    for j in range(ndq):
+        local(('dq', j), wdq_h.at[pl.ds(j * krow, krow), pl.ds(pl.multiple_of(c * ucol, LANES), ucol)], wuq_v.at[j], dq_sem.at[j])
     local('gq', gq_h, gq_v, in_sem.at[3])
     local('gkv', gkv_h, gkv_v, in_sem.at[4])
     local('freq', freq_h, freq_v, in_sem.at[5])
-    ucol = 768
-    nuq = wuq_v.shape[1] // ucol
-    for s in range(nslab):
-        local(('uk', s), wuk_h.at[:, pl.ds(pl.multiple_of(c * half_heads + s * slab, slab), slab), :], wuk_v.at[s], uk_sem.at[s])
+    nuq = wuq_h.shape[1] // 2 // ucol
+    uslot = [(ndq + j) % nslot for j in range(nuq)]
+    uks = [(('uk', s), wuk_h.at[:, pl.ds(pl.multiple_of(c * half_heads + s * slab, slab), slab), :], wuk_v.at[s], uk_sem.at[s])
+           for s in range(nslab)]
+    later.append([('dkv', wdkv_h.at[:, pl.ds(pl.multiple_of(gi * kdkv, LANES), kdkv)], wdkv_v, in_sem.at[2])] + uks[:nslab // 2])
+    later.append(uks[nslab // 2:])
     for j in range(nuq):
         later.append([(('uq', j), wuq_h.at[:, pl.ds(pl.multiple_of(c * nuq * ucol + j * ucol, LANES), ucol)],
-                       wuq_v.at[:, pl.ds(j * ucol, ucol)], uq_sem.at[j])])
+                       wuq_v.at[uslot[j]], uq_sem.at[j])])
     for b in range(nreq):
         later.append([(('cc', b), cc_h.at[b], cc_v.at[b], cc_sem.at[0, b]), (('kr', b), kr_h.at[b], kr_v.at[b], cc_sem.at[1, b])])
     head0 = c * half_heads + xx * slab + yy * own
@@ -134,11 +137,19 @@
         pl.semaphore_signal(barrier, inc=1, device_id={'cp': base + 2 * i + oc}, device_id_type=MESH)
 
     done('x')
-    done('dq')
-    part = dot(x_v[:, pl.ds(pl.multiple_of(c * kdq, kdq), kdq)], wdq_v[...])
-    cqp_v[gi] = part
+    part = None
+    for j in range(ndq):
+        done(('dq', j))
+        pj = dot(x_v[:, j * krow:(j + 1) * krow], wuq_v[j])
+        part = pj if part is None else part + pj
+        issue(1)
+    cq_v[c] = part
+    pl.semaphore_wait(barrier, chips - 1 + side)
+    cq_copy = pltpu.make_async_remote_copy(src_ref=cq_v.at[c], dst_ref=cq_v.at[c], send_sem=a_send, recv_sem=a_recv,
+                                           device_id={'cp': partner}, device_id_type=MESH)
+    cq_copy.start()
     issue(2)
-    pl.semaphore_wait(barrier, chips - 1 + side)
+    pending['cq'] = cq_copy.wait
 
     def to_ring(buf, send, recv):
         def go(r, _):
@@ -148,18 +159,12 @@
             return 0
         lax.fori_loop(1, inner, go, 0)
 
-    to_ring(cqp_v, a_send, a_recv)
-    issue(1)
-    pending['a_send'] = lambda: wait_bytes(cqp_v.at[pl.ds(0, inner - 1)], a_send)
-    pending['a_recv'] = lambda: wait_bytes(cqp_v.at[pl.ds(0, inner - 1)], a_recv)
     done('dkv')
     kvp_v[gi, :, 0:latent + rope] = dot_nt(x_v[:, pl.ds(pl.multiple_of(gi * kdkv, LANES), kdkv)], wdkv_v[...])
     kvp_v[gi, :, latent + rope:] = jnp.zeros((nreq, wide - latent - rope), F32)
     to_ring(kvp_v, kv_send, kv_recv)
     pending['kv_send'] = lambda: wait_bytes(kvp_v.at[pl.ds(0, inner - 1)], kv_send)
     pending['kv_recv'] = lambda: wait_bytes(kvp_v.at[pl.ds(0, inner - 1)], kv_recv)
-
-    issue(1)
 
     xall = x_v[...].astype(F32)
     for i in range(2):
@@ -181,14 +186,13 @@
 
     for s in range(nslab):
         done(('uk', s))
+        widen(wuk_v.at[s])
         issue(1)
-        widen(wuk_v.at[s])
         for i in range(slab):
             wk_v[s * slab + i] = stage_v[pl.ds(i, latent, stride=slab), :].astype(BF16)
 
-    done('a_recv')
-    cols = [cqp_v[2 * i] + cqp_v[2 * i + 1] for i in range(side)]
-    cq = rounded(jnp.concatenate(cols, axis=1))
+    done('cq')
+    cq = rounded(jnp.concatenate([cq_v[0], cq_v[1]], axis=1))
     done('gq')
     mean_sq = jnp.mean(cq * cq, axis=1, keepdims=True)
     cn = (cq * lax.rsqrt(mean_sq + NORM_EPS) * gq_v[...].reshape(1, gq_v.shape[0])).astype(BF16)
@@ -201,10 +205,7 @@
         return pltpu.make_async_remote_copy(src_ref=view, dst_ref=view, send_sem=q_send.at[s], recv_sem=q_recv.at[s],
                                             device_id={'cp': partner}, device_id_type=MESH)
 
-    for j in range(nuq):
-        done(('uq', j))
-        issue(1)
-        qc = rounded(dot(cn, wuq_v[:, j * ucol:(j + 1) * ucol]))
+    def q_latent(j, qc):
         for i in range(per):
             h = j * per + i
             r = pl.multiple_of(row0 + h * nreq, nreq)
@@ -218,6 +219,14 @@
             q_slab_copy(s).start()
             pending['q', s] = q_slab_copy(s).wait
 
+    qc = None
+    for j in range(nuq):
+        done(('uq', j))
+        issue(1)
+        last, qc = qc, rounded(dot(cn, wuq_v[uslot[j]]))
+        if j > 0:
+            q_latent(j - 1, last)
+    q_latent(nuq - 1, qc)
     issue(len(later))
 
     done('kv_recv')
@@ -239,7 +248,6 @@
 
     scale = (nope + rope) ** -0.5
     block0 = d * tdev
-    key_pos = lax.broadcasted_iota(jnp.int32, (heads, tdev), 1)
     head_row = lax.broadcasted_iota(jnp.int32, (heads, 1), 0)
     mine0 = pl.multiple_of(c * half_heads, half_heads)
     theirs0 = pl.multiple_of(oc * half_heads, half_heads)
@@ -249,28 +257,49 @@
                                             send_sem=pair_send.at[b], recv_sem=pair_recv.at[b],
                                             device_id={'cp': partner}, device_id_type=MESH)
 
-    def attend(b):
-        pltpu.make_async_copy(cc_v.at[b], cc_v.at[b], cc_sem.at[0, b]).wait()
-        pltpu.make_async_copy(kr_v.at[b], kr_v.at[b], cc_sem.at[1, b]).wait()
-        qf = jnp.concatenate([q_v[k, pl.ds(b, heads, stride=nreq), :] for k in range(wide // LANES)], axis=1)
-        qb = qf.astype(BF16)
-        s = (dot_nt(qb[:, :latent], cc_v[b]) + dot(qb[:, latent:latent + rope], kr_v[b])) * scale
+    nkc = 4
+    kc = tdev // nkc
+    half_lane = lax.broadcasted_iota(jnp.int32, (heads, LANES), 1) < LANES // 2
+    chunk_pos = lax.broadcasted_iota(jnp.int32, (heads, kc), 1)
+
+    def q_of(b):
+        return jnp.concatenate([q_v[k, pl.ds(b, heads, stride=nreq), :] for k in range(wide // LANES)], axis=1)
+
+    def block_ready(b):
+        done(('cc', b))
+        done(('kr', b))
+
+    def scores(b, s_ref):
+        qb = q_of(b).astype(BF16)
         left = ctx_s[b] - block0
-        s = jnp.where(key_pos < left, s, MASKED)
-        new_row = cnf_v[pl.ds(b, 1), :]
+        m = None
+        for k in range(nkc):
+            cols = slice(k * kc, (k + 1) * kc)
+            s = (dot_nt(qb[:, :latent], cc_v[b, cols]) + dot(qb[:, latent:latent + rope], kr_v[b, :, cols])) * scale
+            s = jnp.where(chunk_pos < left - k * kc, s, MASKED)
+            s_ref[:, cols] = s
+            mk = jnp.max(s, axis=1, keepdims=True)
+            m = mk if m is None else jnp.maximum(m, mk)
+        m_v[b] = jnp.broadcast_to(m, (heads, LANES))
+
+    def weigh(b, s_ref):
+        qf = q_of(b)
+        left = ctx_s[b] - block0
+        new_row = cnf_v[b:b + 1, :]
         new_s = jnp.sum(qf * new_row, axis=1, keepdims=True) * scale
         at = head_row * 0 + left
-        owner = jnp.logical_and(at >= 0, at < tdev)
-        new_s = jnp.where(owner, new_s, MASKED)
-        m = jnp.maximum(jnp.maximum(jnp.max(s, axis=1, keepdims=True), new_s), FLOOR)
-        p = jnp.exp(s - m)
+        new_s = jnp.where(jnp.logical_and(at >= 0, at < tdev), new_s, MASKED)
+        m = jnp.maximum(jnp.maximum(m_v[b][:, :1], new_s), FLOOR)
         new_w = jnp.exp(new_s - m)
-        l = jnp.sum(p, axis=1, keepdims=True) + new_w
-        acc = dot(p.astype(BF16), cc_v[b]) + rounded(new_w) * new_row[:, :latent]
+        l = new_w
+        acc = rounded(new_w) * new_row[:, :latent]
+        for k in range(nkc):
+            cols = slice(k * kc, (k + 1) * kc)
+            p = jnp.exp(s_ref[:, cols] - m)
+            l = l + jnp.sum(p, axis=1, keepdims=True)
+            acc = acc + dot(p.astype(BF16), cc_v[b, cols])
         acc_v[b, :, :latent] = acc
-        ml_lane = lax.broadcasted_iota(jnp.int32, (heads, LANES), 1)
-        acc_v[b, :, latent:] = jnp.where(ml_lane < LANES // 2, m, l)
-        pair_copy(b).start()
+        acc_v[b, :, latent:] = jnp.where(half_lane, m, l)
 
     quarter = half_heads // side
 
@@ -302,50 +331,57 @@
         return jnp.where(side_lane < LANES // 2, m, l)
 
     def pair_merge(b):
-        pair_copy(b).wait_recv()
         m, l, acc = merge([acc_v[b, pl.ds(mine0, half_heads), :], pair_v[b]])
         xs_v[b, :, :latent] = acc
         xs_v[b, :, latent:] = with_ml(m, l)
+
+    def pair_sent(b):
         for r in range(1, side):
             xs_copy(b, r).start()
 
     def ring_merge(b):
-        wait_bytes(xsr_v.at[b], xs_recv.at[b])
         mine = xs_v[b, pl.ds(pl.multiple_of(xx * quarter, quarter), quarter), :]
         m, l, acc = merge([mine] + [xsr_v[b, r] for r in range(side - 1)])
         ml = with_ml(m, l)
         for k in range(side):
             ys_v[b, k, :, :latent] = acc[own * k:own * (k + 1), :]
             ys_v[b, k, :, latent:] = ml[own * k:own * (k + 1), :]
+
+    def ring_sent(b):
         for r in range(1, side):
             ys_copy(b, r).start()
 
-    lag = 4
-
-    def attend_step(b, _):
-        attend(b)
-
-        @pl.when(b > 0)
-        def _():
+    lag = 5
+    s_bufs = (sa_v, sb_v)
+    block_ready(0)
+    scores(0, s_bufs[0])
+    for b in range(nreq):
+        if b + 1 < nreq:
+            block_ready(b + 1)
+        if b > 0:
+            pair_copy(b - 1).wait_recv()
+        if b >= lag:
+            wait_bytes(xsr_v.at[b - lag], xs_recv.at[b - lag])
+        if b + 1 < nreq:
+            scores(b + 1, s_bufs[(b + 1) % 2])
+        weigh(b, s_bufs[b % 2])
+        if b > 0:
             pair_merge(b - 1)
-
-        @pl.when(b >= lag)
-        def _():
+        if b >= lag:
             ring_merge(b - lag)
-        return 0
-
-    lax.fori_loop(0, nreq, attend_step, 0)
-    for b in range(nreq):
-        pending.pop(('cc', b))
-        pending.pop(('kr', b))
+        pair_copy(b).start()
         pending['pair', b] = pair_copy(b).wait_send
+        if b > 0:
+            pair_sent(b - 1)
+        if b >= lag:
+            ring_sent(b - lag)
+    pair_copy(nreq - 1).wait_recv()
     pair_merge(nreq - 1)
-
-    def ring_step(b, _):
+    pair_sent(nreq - 1)
+    for b in range(nreq - lag, nreq):
+        wait_bytes(xsr_v.at[b], xs_recv.at[b])
         ring_merge(b)
-        return 0
-
-    lax.fori_loop(nreq - lag, nreq, ring_step, 0)
+        ring_sent(b)
 
     def each(view, sem):
         def go(b, _):
@@ -452,19 +488,20 @@
         out_shape = (jax.ShapeDtypeStruct((nreq, dmodel), BF16), jax.ShapeDtypeStruct((nreq, latent), BF16),
                      jax.ShapeDtypeStruct((nreq, rope), BF16))
         scratch = [
-            vm((nreq, dmodel), BF16), vm((dmodel // 2, qlora // side), BF16), vm((qlora,), F32),
-            vm((qlora, w_uq.shape[1] // 2), BF16), vm((w_dkv.shape[1], dmodel // inner), BF16), vm((1, latent), F32),
+            vm((nreq, dmodel), BF16), vm((qlora,), F32),
+            vm((w_uq.shape[1] // qlora, qlora, qlora // 2), BF16), vm((w_dkv.shape[1], dmodel // inner), BF16), vm((1, latent), F32),
             vm((half // 8, latent, 8, nope), BF16), vm((latent, 8, nope), BF16), vm((own * nope, dmodel), BF16),
             vm((nreq, tdev, latent), BF16), vm((nreq, rope, tdev), BF16), vm((1, LANES), F32), vm((own, latent, nope), BF16),
             vm((half, latent, nope), BF16), vm((latent * 8, nope), F32),
-            vm((2, nreq // 2, dmodel), F32), vm((inner, nreq, qlora // side), F32), vm((inner, nreq, wide), F32),
+            vm((2, nreq // 2, dmodel), F32), vm((2, nreq, qlora // 2), F32), vm((inner, nreq, wide), F32),
             vm((wide // LANES, heads * nreq, LANES), F32), vm((nreq, wide), F32),
+            vm((heads, tdev), F32), vm((heads, tdev), F32), vm((nreq, heads, LANES), F32),
             vm((nreq, heads, wide), F32), vm((nreq, half, wide), F32),
             vm((nreq, half, wide), F32), vm((nreq, side - 1, half // side, wide), F32),
             vm((nreq, side, own, wide), F32), vm((nreq, side - 1, own, wide), F32), vm((own, nreq, latent), F32),
             vm((2, nreq // 2, dmodel), F32), vm((nreq // 2, dmodel), F32),
             vm((chips, nreq // 2, tcol), F32), vm((chips - 1, nreq // 2, tcol), F32), vm((2, chips, nreq // 2, tcol), F32),
-            dma((8,)), dma((w_uq.shape[1] // 2 // 768,)), dma((half // 8,)), dma((2, nreq)),
+            dma((8,)), dma((dmodel // qlora,)), dma((w_uq.shape[1] // qlora,)), dma((half // 8,)), dma((2, nreq)),
             dma, dma, dma, dma, dma((half // 8,)), dma((half // 8,)), dma((nreq,)), dma((nreq,)), dma((nreq,)), dma((nreq,)), dma((nreq,)), dma((nreq,)),
             dma, dma, dma, dma, dma, dma, dma, dma,
         ]

time: 58.4 us -> 62.8 us (1.075)
  Pallas kernels: 57.6 us -> 62 us
    pallas_call x1, Pallas kernels: 56.1 us -> 60.5 us  [decode_step(): pl.pallas_call(functools.partial(step_kernel, (cp, side)), out_shape=jax....]
where the time goes in v3:
time: 62.8 us; the launch traced here: 62.7 us
  Pallas kernels  62 us (99%)
  between operations  0.64 us (1%)
    pallas_call x1, Pallas kernels, decode_step(): pl.pallas_call(functools.partial(step_kernel, (cp, side)), out_shape=jax....  60.5 us
    pallas_call x1, Pallas kernels, decode_step(): pl.pallas_call(split_outputs, out_shape=out_shape, in_specs=[vspec], out_...  1.55 us

profile of v3, /device:TPU:97, one launch (start us, length us, event | category | flops | bytes accessed | tf_op | source)
XLA Modules:
  0.0 62.7 jit_solution(9003956488230980563)
XLA Ops:
  0.6 60.5 %decode_step.1.packed_v = bf16[8,6784]{1,0:T(8,128)(2,1)} custom-call(bf16[8,6144]{1,0:T(8,128)(2,1)} %x_h.1, bf16[6144,1536]{1,0:T(8,128)(2,1)} %wdq_h.1, f32[1536]{0:T(1024)} %gq_h.1, bf16[1536,12288]{1,0:T(8,128)(2,1)} %wuq_h.1, bf16[576,6144]{1,0:T(8,128)(2,1)} %bitcast.3, f32[1,512]{1,0:T(1,128)} %bitcast.5, bf16[512,64,128]{2,1,0:T(8,128)(2,1)} %wuk_h.1, ...), custom_call_target="tpu_custom_call" | custom-call | tf_op jit(solution)/shard_map/decode_step/pallas_call | solution.py:508
  61.1 1.5 %split_outputs.1 = (bf16[8,6144]{1,0:T(8,128)(2,1)}, bf16[8,512]{1,0:T(8,128)(2,1)}, bf16[8,64]{1,0:T(8,128)(2,1)}) custom-call(bf16[8,6784]{1,0:T(8,128)(2,1)} %decode_step.1.packed_v), custom_call_target="tpu_custom_call" | custom-call | tf_op jit(solution)/shard_map/split_outputs/pallas_call | solution.py:519

commit v4 on v3

--- a/solution.py
+++ b/solution.py
@@ -94,37 +94,40 @@
         cpy.start()
         pending[name] = cpy.wait
 
-    later = []
-
-    def issue(n):
-        for _ in range(min(n, len(later))):
-            for args in later.pop(0):
-                local(*args)
-
     local('x', x_h, x_v, in_sem.at[0])
     nslot, krow, ucol = wuq_v.shape
     ndq = dmodel // krow
     for j in range(ndq):
-        local(('dq', j), wdq_h.at[pl.ds(j * krow, krow), pl.ds(pl.multiple_of(c * ucol, LANES), ucol)], wuq_v.at[j], dq_sem.at[j])
+        pltpu.make_async_copy(wdq_h.at[pl.ds(j * krow, krow), pl.ds(pl.multiple_of(c * ucol, LANES), ucol)],
+                              wuq_v.at[j], dq_sem.at[j]).start()
     local('gq', gq_h, gq_v, in_sem.at[3])
     local('gkv', gkv_h, gkv_v, in_sem.at[4])
     local('freq', freq_h, freq_v, in_sem.at[5])
     nuq = wuq_h.shape[1] // 2 // ucol
-    uslot = [(ndq + j) % nslot for j in range(nuq)]
-    uks = [(('uk', s), wuk_h.at[:, pl.ds(pl.multiple_of(c * half_heads + s * slab, slab), slab), :], wuk_v.at[s], uk_sem.at[s])
-           for s in range(nslab)]
-    later.append([('dkv', wdkv_h.at[:, pl.ds(pl.multiple_of(gi * kdkv, LANES), kdkv)], wdkv_v, in_sem.at[2])] + uks[:nslab // 2])
-    later.append(uks[nslab // 2:])
-    for j in range(nuq):
-        later.append([(('uq', j), wuq_h.at[:, pl.ds(pl.multiple_of(c * nuq * ucol + j * ucol, LANES), ucol)],
-                       wuq_v.at[uslot[j]], uq_sem.at[j])])
-    for b in range(nreq):
-        later.append([(('cc', b), cc_h.at[b], cc_v.at[b], cc_sem.at[0, b]), (('kr', b), kr_h.at[b], kr_v.at[b], cc_sem.at[1, b])])
+
+    def uq_copy(j):
+        return pltpu.make_async_copy(wuq_h.at[:, pl.ds(pl.multiple_of((c * nuq + j) * ucol, LANES), ucol)],
+                                     wuq_v.at[lax.rem(ndq + j, nslot)], uq_sem.at[j])
+
+    def uk_copy(s):
+        return pltpu.make_async_copy(wuk_h.at[:, pl.ds(pl.multiple_of(c * half_heads + s * slab, slab), slab), :],
+                                     wuk_v.at[s], uk_sem.at[s])
+
+    def cache_copies(b):
+        return (pltpu.make_async_copy(cc_h.at[b], cc_v.at[b], cc_sem.at[0, b]),
+                pltpu.make_async_copy(kr_h.at[b], kr_v.at[b], cc_sem.at[1, b]))
+
+    def cache_start(b):
+        for cpy in cache_copies(b):
+            cpy.start()
+
+    def cache_wait(b):
+        for cpy in cache_copies(b):
+            cpy.wait()
+
     head0 = c * half_heads + xx * slab + yy * own
     head_slab = head0 // slab
     head_in = head0 - head_slab * slab
-    later.append([('uv', wuv_h.at[:, pl.ds(pl.multiple_of(head_slab * slab, slab), slab), :], wuv_v, in_sem.at[6])])
-    later.append([('wo', wo_h.at[pl.ds(pl.multiple_of(head0 * nope, own * nope), own * nope), :], wo_v, in_sem.at[7])])
 
     barrier = pltpu.get_barrier_semaphore()
 
@@ -137,18 +140,26 @@
         pl.semaphore_signal(barrier, inc=1, device_id={'cp': base + 2 * i + oc}, device_id_type=MESH)
 
     done('x')
-    part = None
-    for j in range(ndq):
-        done(('dq', j))
-        pj = dot(x_v[:, j * krow:(j + 1) * krow], wuq_v[j])
-        part = pj if part is None else part + pj
-        issue(1)
+    local('dkv', wdkv_h.at[:, pl.ds(pl.multiple_of(gi * kdkv, LANES), kdkv)], wdkv_v, in_sem.at[2])
+    for s in range(nslab):
+        uk_copy(s).start()
+
+    def a_step(j, part):
+        pltpu.make_async_copy(wuq_v.at[j], wuq_v.at[j], dq_sem.at[j]).wait()
+
+        @pl.when(j >= 2)
+        def _():
+            uq_copy(j - 2).start()
+        return part + dot(x_v[:, pl.ds(pl.multiple_of(j * krow, krow), krow)], wuq_v[j])
+
+    part = lax.fori_loop(0, ndq, a_step, jnp.zeros((nreq, ucol), F32))
     cq_v[c] = part
     pl.semaphore_wait(barrier, chips - 1 + side)
     cq_copy = pltpu.make_async_remote_copy(src_ref=cq_v.at[c], dst_ref=cq_v.at[c], send_sem=a_send, recv_sem=a_recv,
                                            device_id={'cp': partner}, device_id_type=MESH)
     cq_copy.start()
-    issue(2)
+    for j in range(ndq - 2, nslot - ndq):
+        uq_copy(j).start()
     pending['cq'] = cq_copy.wait
 
     def to_ring(buf, send, recv):
@@ -184,12 +195,18 @@
         swapped = jnp.concatenate([v[:, half_rope:], v[:, :half_rope]], axis=1)
         return v * cos_full + swapped * sin_full
 
-    for s in range(nslab):
-        done(('uk', s))
+    def uk_step(s, _):
+        uk_copy(s).wait()
+        uq_copy(nslot - ndq + s).start()
         widen(wuk_v.at[s])
-        issue(1)
-        for i in range(slab):
+
+        def head_step(i, _):
             wk_v[s * slab + i] = stage_v[pl.ds(i, latent, stride=slab), :].astype(BF16)
+            return 0
+        lax.fori_loop(0, slab, head_step, 0)
+        return 0
+
+    lax.fori_loop(0, nslab, uk_step, 0)
 
     done('cq')
     cq = rounded(jnp.concatenate([cq_v[0], cq_v[1]], axis=1))
@@ -214,20 +231,26 @@
             ql = rounded(dot_nt(qc[:, i * qk:i * qk + nope].astype(BF16), wk_v[h]))
             for k in range(latent // LANES):
                 q_v[k, pl.ds(r, nreq), :] = ql[:, k * LANES:(k + 1) * LANES]
-        if (j + 1) * per % slab == 0:
-            s = (j + 1) * per // slab - 1
-            q_slab_copy(s).start()
-            pending['q', s] = q_slab_copy(s).wait
-
-    qc = None
-    for j in range(nuq):
-        done(('uq', j))
-        issue(1)
-        last, qc = qc, rounded(dot(cn, wuq_v[uslot[j]]))
-        if j > 0:
-            q_latent(j - 1, last)
+    def b_step(j, last):
+        uq_copy(j).wait()
+        cache_start(j - 1)
+        qc = rounded(dot(cn, wuq_v[lax.rem(ndq + j, nslot)]))
+        q_latent(j - 1, last)
+
+        @pl.when(lax.rem(j * per, slab) == 0)
+        def _():
+            q_slab_copy(j * per // slab - 1).start()
+        return qc
+
+    uq_copy(0).wait()
+    qc = lax.fori_loop(1, nuq, b_step, rounded(dot(cn, wuq_v[ndq])))
+    cache_start(nuq - 1)
     q_latent(nuq - 1, qc)
-    issue(len(later))
+    q_slab_copy(nslab - 1).start()
+    for s in range(nslab):
+        pending['q', s] = q_slab_copy(s).wait
+    local('uv', wuv_h.at[:, pl.ds(pl.multiple_of(head_slab * slab, slab), slab), :], wuv_v, in_sem.at[6])
+    local('wo', wo_h.at[pl.ds(pl.multiple_of(head0 * nope, own * nope), own * nope), :], wo_v, in_sem.at[7])
 
     done('kv_recv')
     kv = kvp_v[0]
@@ -265,10 +288,6 @@
     def q_of(b):
         return jnp.concatenate([q_v[k, pl.ds(b, heads, stride=nreq), :] for k in range(wide // LANES)], axis=1)
 
-    def block_ready(b):
-        done(('cc', b))
-        done(('kr', b))
-
     def scores(b, s_ref):
         qb = q_of(b).astype(BF16)
         left = ctx_s[b] - block0
@@ -285,7 +304,7 @@
     def weigh(b, s_ref):
         qf = q_of(b)
         left = ctx_s[b] - block0
-        new_row = cnf_v[b:b + 1, :]
+        new_row = cnf_v[pl.ds(b, 1), :]
         new_s = jnp.sum(qf * new_row, axis=1, keepdims=True) * scale
         at = head_row * 0 + left
         new_s = jnp.where(jnp.logical_and(at >= 0, at < tdev), new_s, MASKED)
@@ -351,37 +370,46 @@
         for r in range(1, side):
             ys_copy(b, r).start()
 
-    lag = 5
-    s_bufs = (sa_v, sb_v)
-    block_ready(0)
-    scores(0, s_bufs[0])
+    def pair_step(b):
+        pair_copy(b).wait_recv()
+        pair_merge(b)
+        pair_sent(b)
+
+    def two_requests(i, _):
+        b = 2 * i
+        cache_wait(b + 1)
+        scores(b + 1, sb_v)
+        weigh(b, sa_v)
+        pair_copy(b).start()
+
+        @pl.when(i > 0)
+        def _():
+            pair_step(b - 1)
+
+        @pl.when(b + 2 < nreq)
+        def _():
+            cache_wait(b + 2)
+        scores(jnp.minimum(b + 2, nreq - 1), sa_v)
+        weigh(b + 1, sb_v)
+        pair_copy(b + 1).start()
+        pair_step(b)
+        return 0
+
+    cache_wait(0)
+    scores(0, sa_v)
+    lax.fori_loop(0, nreq // 2, two_requests, 0)
     for b in range(nreq):
-        if b + 1 < nreq:
-            block_ready(b + 1)
-        if b > 0:
-            pair_copy(b - 1).wait_recv()
-        if b >= lag:
-            wait_bytes(xsr_v.at[b - lag], xs_recv.at[b - lag])
-        if b + 1 < nreq:
-            scores(b + 1, s_bufs[(b + 1) % 2])
-        weigh(b, s_bufs[b % 2])
-        if b > 0:
-            pair_merge(b - 1)
-        if b >= lag:
-            ring_merge(b - lag)
-        pair_copy(b).start()
         pending['pair', b] = pair_copy(b).wait_send
-        if b > 0:
-            pair_sent(b - 1)
-        if b >= lag:
-            ring_sent(b - lag)
-    pair_copy(nreq - 1).wait_recv()
-    pair_merge(nreq - 1)
-    pair_sent(nreq - 1)
-    for b in range(nreq - lag, nreq):
+
+    def ring_step(b, _):
         wait_bytes(xsr_v.at[b], xs_recv.at[b])
         ring_merge(b)
         ring_sent(b)
+        return 0
+
+    lax.fori_loop(0, 2, ring_step, 0)
+    pair_step(nreq - 1)
+    lax.fori_loop(2, nreq, ring_step, 0)
 
     def each(view, sem):
         def go(b, _):

time: 62.8 us -> 59 us (0.939)
  Pallas kernels: 62 us -> 58.2 us
    pallas_call x1, Pallas kernels: 60.5 us -> 56.7 us  [decode_step(): pl.pallas_call(functools.partial(step_kernel, (cp, side)), out_shape=jax....]
where the time goes in v4:
time: 59 us; the launch traced here: 58.8 us
  Pallas kernels  58.2 us (99%)
  between operations  0.64 us (1%)
    pallas_call x1, Pallas kernels, decode_step(): pl.pallas_call(functools.partial(step_kernel, (cp, side)), out_shape=jax....  56.7 us
    pallas_call x1, Pallas kernels, decode_step(): pl.pallas_call(split_outputs, out_shape=out_shape, in_specs=[vspec], out_...  1.55 us

profile of v4, /device:TPU:97, one launch (start us, length us, event | category | flops | bytes accessed | tf_op | source)
XLA Modules:
  0.0 58.8 jit_solution(3277112208575463753)
XLA Ops:
  0.6 56.7 %decode_step.1.packed_v = bf16[8,6784]{1,0:T(8,128)(2,1)} custom-call(bf16[8,6144]{1,0:T(8,128)(2,1)} %x_h.1, bf16[6144,1536]{1,0:T(8,128)(2,1)} %wdq_h.1, f32[1536]{0:T(1024)} %gq_h.1, bf16[1536,12288]{1,0:T(8,128)(2,1)} %wuq_h.1, bf16[576,6144]{1,0:T(8,128)(2,1)} %bitcast.3, f32[1,512]{1,0:T(1,128)} %bitcast.5, bf16[512,64,128]{2,1,0:T(8,128)(2,1)} %wuk_h.1, ...), custom_call_target="tpu_custom_call" | custom-call | tf_op jit(solution)/shard_map/decode_step/pallas_call | solution.py:536
  57.3 1.5 %split_outputs.1 = (bf16[8,6144]{1,0:T(8,128)(2,1)}, bf16[8,512]{1,0:T(8,128)(2,1)}, bf16[8,64]{1,0:T(8,128)(2,1)}) custom-call(bf16[8,6784]{1,0:T(8,128)(2,1)} %decode_step.1.packed_v), custom_call_target="tpu_custom_call" | custom-call | tf_op jit(solution)/shard_map/split_outputs/pallas_call | solution.py:547

commit v5 on v4

--- a/solution.py
+++ b/solution.py
@@ -322,17 +322,26 @@
 
     quarter = half_heads // side
 
-    def xs_copy(b, r):
-        px = lax.rem(xx + r, side)
-        return pltpu.make_async_remote_copy(src_ref=xs_v.at[b, pl.ds(pl.multiple_of(px * quarter, quarter), quarter)],
+    def ring_peer(axis, r):
+        if axis == 0:
+            p = lax.rem(xx + r, side)
+            return p, base + 2 * p + c
+        p = lax.rem(yy + r, side)
+        return p, p * inner + gi
+
+    here = (xx, yy)
+
+    def xs_copy(b, axis, r):
+        p, dev = ring_peer(axis, r)
+        return pltpu.make_async_remote_copy(src_ref=xs_v.at[b, pl.ds(pl.multiple_of(p * quarter, quarter), quarter)],
                                             dst_ref=xsr_v.at[b, r - 1], send_sem=xs_send.at[b], recv_sem=xs_recv.at[b],
-                                            device_id={'cp': base + 2 * px + c}, device_id_type=MESH)
-
-    def ys_copy(b, r):
-        py = lax.rem(yy + r, side)
-        return pltpu.make_async_remote_copy(src_ref=ys_v.at[b, py], dst_ref=ysr_v.at[b, r - 1],
+                                            device_id={'cp': dev}, device_id_type=MESH)
+
+    def ys_copy(b, axis, r):
+        p, dev = ring_peer(1 - axis, r)
+        return pltpu.make_async_remote_copy(src_ref=ys_v.at[b, p], dst_ref=ysr_v.at[b, r - 1],
                                             send_sem=ys_send.at[b], recv_sem=ys_recv.at[b],
-                                            device_id={'cp': py * inner + gi}, device_id_type=MESH)
+                                            device_id={'cp': dev}, device_id_type=MESH)
 
     def ml_of(v):
         return v[:, latent:latent + 1], v[:, wide - 1:wide]
@@ -349,31 +358,30 @@
         side_lane = lax.broadcasted_iota(jnp.int32, (m.shape[0], LANES), 1)
         return jnp.where(side_lane < LANES // 2, m, l)
 
-    def pair_merge(b):
+    def pair_step(b, axis):
+        pair_copy(b).wait_recv()
         m, l, acc = merge([acc_v[b, pl.ds(mine0, half_heads), :], pair_v[b]])
-        xs_v[b, :, :latent] = acc
-        xs_v[b, :, latent:] = with_ml(m, l)
-
-    def pair_sent(b):
+        ml = with_ml(m, l)
+        if axis == 0:
+            xs_v[b, :, :latent] = acc
+            xs_v[b, :, latent:] = ml
+        else:
+            for p in range(side):
+                for k in range(side):
+                    src = slice(p * quarter + k * own, p * quarter + (k + 1) * own)
+                    dst = slice(k * quarter + p * own, k * quarter + (p + 1) * own)
+                    xs_v[b, dst, :latent] = acc[src]
+                    xs_v[b, dst, latent:] = ml[src]
         for r in range(1, side):
-            xs_copy(b, r).start()
-
-    def ring_merge(b):
-        mine = xs_v[b, pl.ds(pl.multiple_of(xx * quarter, quarter), quarter), :]
+            xs_copy(b, axis, r).start()
+
+    def ring_merge(b, axis):
+        mine = xs_v[b, pl.ds(pl.multiple_of(here[axis] * quarter, quarter), quarter), :]
         m, l, acc = merge([mine] + [xsr_v[b, r] for r in range(side - 1)])
         ml = with_ml(m, l)
         for k in range(side):
             ys_v[b, k, :, :latent] = acc[own * k:own * (k + 1), :]
             ys_v[b, k, :, latent:] = ml[own * k:own * (k + 1), :]
-
-    def ring_sent(b):
-        for r in range(1, side):
-            ys_copy(b, r).start()
-
-    def pair_step(b):
-        pair_copy(b).wait_recv()
-        pair_merge(b)
-        pair_sent(b)
 
     def two_requests(i, _):
         b = 2 * i
@@ -384,7 +392,7 @@
 
         @pl.when(i > 0)
         def _():
-            pair_step(b - 1)
+            pair_step(b - 1, 1)
 
         @pl.when(b + 2 < nreq)
         def _():
@@ -392,7 +400,7 @@
         scores(jnp.minimum(b + 2, nreq - 1), sa_v)
         weigh(b + 1, sb_v)
         pair_copy(b + 1).start()
-        pair_step(b)
+        pair_step(b, 0)
         return 0
 
     cache_wait(0)
@@ -401,15 +409,19 @@
     for b in range(nreq):
         pending['pair', b] = pair_copy(b).wait_send
 
-    def ring_step(b, _):
-        wait_bytes(xsr_v.at[b], xs_recv.at[b])
-        ring_merge(b)
-        ring_sent(b)
+    def ring_step(i, _):
+        for k in range(2):
+            wait_bytes(xsr_v.at[2 * i + k], xs_recv.at[2 * i + k])
+        for k in range(2):
+            ring_merge(2 * i + k, k)
+        for k in range(2):
+            for r in range(1, side):
+                ys_copy(2 * i + k, k, r).start()
         return 0
 
-    lax.fori_loop(0, 2, ring_step, 0)
-    pair_step(nreq - 1)
-    lax.fori_loop(2, nreq, ring_step, 0)
+    lax.fori_loop(0, 1, ring_step, 0)
+    pair_step(nreq - 1, 1)
+    lax.fori_loop(1, nreq // 2, ring_step, 0)
 
     def each(view, sem):
         def go(b, _):
@@ -426,16 +438,12 @@
     for k in range(own):
         wv_v[k] = stage_v[pl.ds(head_in + k, latent, stride=slab), :].astype(BF16)
 
-    def owner_merge(b, _):
-        wait_bytes(ysr_v.at[b], ys_recv.at[b])
-        m, l, acc = merge([ys_v[b, yy]] + [ysr_v[b, r] for r in range(side - 1)])
+    done('ys_recv')
+    for b in range(nreq):
+        m, l, acc = merge([ys_v[b, here[1 - b % 2]]] + [ysr_v[b, r] for r in range(side - 1)])
         ol = rounded(acc / l)
         for k in range(own):
-            olat_v[k, pl.ds(b, 1), :] = ol[k:k + 1, :]
-        return 0
-
-    lax.fori_loop(0, nreq, owner_merge, 0)
-    pending.pop('ys_recv')
+            olat_v[k, b:b + 1, :] = ol[k:k + 1, :]
 
     done('wo')
     outs = []

time: 59 us -> 59.2 us (level)
  no operation moved by 1% of the time
where the time goes in v5:
time: 59.2 us; the launch traced here: 59 us
  Pallas kernels  58.4 us (99%)
  between operations  0.64 us (1%)
    pallas_call x1, Pallas kernels, decode_step(): pl.pallas_call(functools.partial(step_kernel, (cp, side)), out_shape=jax....  56.9 us
    pallas_call x1, Pallas kernels, decode_step(): pl.pallas_call(split_outputs, out_shape=out_shape, in_specs=[vspec], out_...  1.55 us

profile of v5, /device:TPU:97, one launch (start us, length us, event | category | flops | bytes accessed | tf_op | source)
XLA Modules:
  0.0 59.0 jit_solution(1822246292807645423)
XLA Ops:
  0.6 56.9 %decode_step.1.packed_v = bf16[8,6784]{1,0:T(8,128)(2,1)} custom-call(bf16[8,6144]{1,0:T(8,128)(2,1)} %x_h.1, bf16[6144,1536]{1,0:T(8,128)(2,1)} %wdq_h.1, f32[1536]{0:T(1024)} %gq_h.1, bf16[1536,12288]{1,0:T(8,128)(2,1)} %wuq_h.1, bf16[576,6144]{1,0:T(8,128)(2,1)} %bitcast.3, f32[1,512]{1,0:T(1,128)} %bitcast.5, bf16[512,64,128]{2,1,0:T(8,128)(2,1)} %wuk_h.1, ...), custom_call_target="tpu_custom_call" | custom-call | tf_op jit(solution)/shard_map/decode_step/pallas_call | solution.py:544
  57.5 1.5 %split_outputs.1 = (bf16[8,6144]{1,0:T(8,128)(2,1)}, bf16[8,512]{1,0:T(8,128)(2,1)}, bf16[8,64]{1,0:T(8,128)(2,1)}) custom-call(bf16[8,6784]{1,0:T(8,128)(2,1)} %decode_step.1.packed_v), custom_call_target="tpu_custom_call" | custom-call | tf_op jit(solution)/shard_map/split_outputs/pallas_call | solution.py:555

commit v6 on v5

--- a/solution.py
+++ b/solution.py
@@ -38,9 +38,9 @@
 def step_kernel(dims, x_h, wdq_h, gq_h, wuq_h, wdkv_h, gkv_h, wuk_h, wuv_h, wo_h, cc_h, kr_h, freq_h, ctx_s,
                 out_v,
                 x_v, gq_v, wuq_v, wdkv_v, gkv_v, wuk_v, wuv_v, wo_v, cc_v, kr_v, freq_v, wv_v, wk_v, stage_v,
-                xf_v, cq_v, kvp_v, q_v, cnf_v, sa_v, sb_v, m_v, acc_v, pair_v, xs_v, xsr_v, ys_v, ysr_v, olat_v, po_v, pop_v, pt_v, ptr_v, ag_v,
+                xf_v, cq_v, kvp_v, q_v, cnf_v, sa_v, sb_v, ma_v, mb_v, acc_v, pair_v, xs_v, xsr_v, ys_v, ysr_v, rs_v, rsr_v, olat_v, po_v, pop_v, pt_v, ptr_v, ag_v,
                 in_sem, dq_sem, uq_sem, uk_sem, cc_sem,
-                a_send, a_recv, kv_send, kv_recv, q_send, q_recv, pair_send, pair_recv, xs_send, xs_recv, ys_send, ys_recv,
+                a_send, a_recv, kv_send, kv_recv, q_send, q_recv, pair_send, pair_recv, xs_send, xs_recv, ys_send, ys_recv, rs_send, rs_recv,
                 po_send, po_recv, pt_send, pt_recv, ag_send, ag_recv, ag2_send, ag2_recv):
     cp, side = dims
     chips = cp // 2
@@ -97,9 +97,6 @@
     local('x', x_h, x_v, in_sem.at[0])
     nslot, krow, ucol = wuq_v.shape
     ndq = dmodel // krow
-    for j in range(ndq):
-        pltpu.make_async_copy(wdq_h.at[pl.ds(j * krow, krow), pl.ds(pl.multiple_of(c * ucol, LANES), ucol)],
-                              wuq_v.at[j], dq_sem.at[j]).start()
     local('gq', gq_h, gq_v, in_sem.at[3])
     local('gkv', gkv_h, gkv_v, in_sem.at[4])
     local('freq', freq_h, freq_v, in_sem.at[5])
@@ -129,6 +126,13 @@
     head_slab = head0 // slab
     head_in = head0 - head_slab * slab
 
+    for s in range(nslab):
+        uk_copy(s).start()
+    for j in range(ndq):
+        pltpu.make_async_copy(wdq_h.at[pl.ds(j * krow, krow), pl.ds(pl.multiple_of(c * ucol, LANES), ucol)],
+                              wuq_v.at[j], dq_sem.at[j]).start()
+    local('dkv', wdkv_h.at[:, pl.ds(pl.multiple_of(gi * kdkv, LANES), kdkv)], wdkv_v, in_sem.at[2])
+
     barrier = pltpu.get_barrier_semaphore()
 
     def greet(r, _):
@@ -139,17 +143,27 @@
     for i in range(side):
         pl.semaphore_signal(barrier, inc=1, device_id={'cp': base + 2 * i + oc}, device_id_type=MESH)
 
+    def uk_step(s, _):
+        uk_copy(s).wait()
+        widen(wuk_v.at[s])
+
+        def head_step(i, _):
+            wk_v[s * slab + i] = stage_v[pl.ds(i, latent, stride=slab), :].astype(BF16)
+            return 0
+        lax.fori_loop(0, slab, head_step, 0)
+        return 0
+
+    lax.fori_loop(0, nslab, uk_step, 0)
+    for j in range(2):
+        uq_copy(j).start()
+
     done('x')
-    local('dkv', wdkv_h.at[:, pl.ds(pl.multiple_of(gi * kdkv, LANES), kdkv)], wdkv_v, in_sem.at[2])
-    for s in range(nslab):
-        uk_copy(s).start()
-
     def a_step(j, part):
         pltpu.make_async_copy(wuq_v.at[j], wuq_v.at[j], dq_sem.at[j]).wait()
 
-        @pl.when(j >= 2)
+        @pl.when(j < nslot - ndq - 2)
         def _():
-            uq_copy(j - 2).start()
+            uq_copy(j + 2).start()
         return part + dot(x_v[:, pl.ds(pl.multiple_of(j * krow, krow), krow)], wuq_v[j])
 
     part = lax.fori_loop(0, ndq, a_step, jnp.zeros((nreq, ucol), F32))
@@ -158,7 +172,7 @@
     cq_copy = pltpu.make_async_remote_copy(src_ref=cq_v.at[c], dst_ref=cq_v.at[c], send_sem=a_send, recv_sem=a_recv,
                                            device_id={'cp': partner}, device_id_type=MESH)
     cq_copy.start()
-    for j in range(ndq - 2, nslot - ndq):
+    for j in range(nslot - ndq, nuq):
         uq_copy(j).start()
     pending['cq'] = cq_copy.wait
 
@@ -194,19 +208,6 @@
     def rope_rotate(v):
         swapped = jnp.concatenate([v[:, half_rope:], v[:, :half_rope]], axis=1)
         return v * cos_full + swapped * sin_full
-
-    def uk_step(s, _):
-        uk_copy(s).wait()
-        uq_copy(nslot - ndq + s).start()
-        widen(wuk_v.at[s])
-
-        def head_step(i, _):
-            wk_v[s * slab + i] = stage_v[pl.ds(i, latent, stride=slab), :].astype(BF16)
-            return 0
-        lax.fori_loop(0, slab, head_step, 0)
-        return 0
-
-    lax.fori_loop(0, nslab, uk_step, 0)
 
     done('cq')
     cq = rounded(jnp.concatenate([cq_v[0], cq_v[1]], axis=1))
@@ -288,7 +289,7 @@
     def q_of(b):
         return jnp.concatenate([q_v[k, pl.ds(b, heads, stride=nreq), :] for k in range(wide // LANES)], axis=1)
 
-    def scores(b, s_ref):
+    def scores(b, s_ref, m_ref):
         qb = q_of(b).astype(BF16)
         left = ctx_s[b] - block0
         m = None
@@ -299,16 +300,16 @@
             s_ref[:, cols] = s
             mk = jnp.max(s, axis=1, keepdims=True)
             m = mk if m is None else jnp.maximum(m, mk)
-        m_v[b] = jnp.broadcast_to(m, (heads, LANES))
-
-    def weigh(b, s_ref):
+        m_ref[...] = jnp.broadcast_to(m, (heads, LANES))
+
+    def weigh(b, s_ref, m_ref):
         qf = q_of(b)
         left = ctx_s[b] - block0
         new_row = cnf_v[pl.ds(b, 1), :]
         new_s = jnp.sum(qf * new_row, axis=1, keepdims=True) * scale
         at = head_row * 0 + left
         new_s = jnp.where(jnp.logical_and(at >= 0, at < tdev), new_s, MASKED)
-        m = jnp.maximum(jnp.maximum(m_v[b][:, :1], new_s), FLOOR)
+        m = jnp.maximum(jnp.maximum(m_ref[:, :1], new_s), FLOOR)
         new_w = jnp.exp(new_s - m)
         l = new_w
         acc = rounded(new_w) * new_row[:, :latent]
@@ -357,6 +358,28 @@
     def with_ml(m, l):
         side_lane = lax.broadcasted_iota(jnp.int32, (m.shape[0], LANES), 1)
         return jnp.where(side_lane < LANES // 2, m, l)
+
+    nring = nreq // 2
+
+    def rs_copy(b, r):
+        p = chip_at(r)
+        return pltpu.make_async_remote_copy(src_ref=rs_v.at[b - nring, lax.rem(p, side) * side + p // side],
+                                            dst_ref=rsr_v.at[b - nring, r - 1],
+                                            send_sem=rs_send.at[b - nring], recv_sem=rs_recv.at[b - nring],
+                                            device_id={'cp': 2 * p + c}, device_id_type=MESH)
+
+    def direct_step(b):
+        pair_copy(b).wait_recv()
+        m, l, acc = merge([acc_v[b, pl.ds(mine0, half_heads), :], pair_v[b]])
+        ml = with_ml(m, l)
+        for k in range(chips):
+            rs_v[b - nring, k, :, :latent] = acc[own * k:own * (k + 1), :]
+            rs_v[b - nring, k, :, latent:] = ml[own * k:own * (k + 1), :]
+
+        def go(r, _):
+            rs_copy(b, r).start()
+            return 0
+        lax.fori_loop(1, chips, go, 0)
 
     def pair_step(b, axis):
         pair_copy(b).wait_recv()
@@ -383,33 +406,7 @@
             ys_v[b, k, :, :latent] = acc[own * k:own * (k + 1), :]
             ys_v[b, k, :, latent:] = ml[own * k:own * (k + 1), :]
 
-    def two_requests(i, _):
-        b = 2 * i
-        cache_wait(b + 1)
-        scores(b + 1, sb_v)
-        weigh(b, sa_v)
-        pair_copy(b).start()
-
-        @pl.when(i > 0)
-        def _():
-            pair_step(b - 1, 1)
-
-        @pl.when(b + 2 < nreq)
-        def _():
-            cache_wait(b + 2)
-        scores(jnp.minimum(b + 2, nreq - 1), sa_v)
-        weigh(b + 1, sb_v)
-        pair_copy(b + 1).start()
-        pair_step(b, 0)
-        return 0
-
-    cache_wait(0)
-    scores(0, sa_v)
-    lax.fori_loop(0, nreq // 2, two_requests, 0)
-    for b in range(nreq):
-        pending['pair', b] = pair_copy(b).wait_send
-
-    def ring_step(i, _):
+    def ring_step(i):
         for k in range(2):
             wait_bytes(xsr_v.at[2 * i + k], xs_recv.at[2 * i + k])
         for k in range(2):
@@ -417,33 +414,76 @@
         for k in range(2):
             for r in range(1, side):
                 ys_copy(2 * i + k, k, r).start()
+
+    def two_requests(i, _):
+        b = 2 * i
+        cache_wait(b + 1)
+        scores(b + 1, sb_v, mb_v)
+        weigh(b, sa_v, ma_v)
+        pair_copy(b).start()
+
+        @pl.when(jnp.logical_and(b - 1 > 0, b - 1 < nring))
+        def _():
+            pair_step(b - 1, 1)
+
+        @pl.when(b - 1 >= nring)
+        def _():
+            direct_step(b - 1)
+
+        @pl.when(b + 2 < nreq)
+        def _():
+            cache_wait(b + 2)
+        scores(jnp.minimum(b + 2, nreq - 1), sa_v, ma_v)
+        weigh(b + 1, sb_v, mb_v)
+        pair_copy(b + 1).start()
+        @pl.when(b < nring)
+        def _():
+            pair_step(b, 0)
+
+        @pl.when(b >= nring)
+        def _():
+            direct_step(b)
+            ring_step(i - nring // 2)
         return 0
 
-    lax.fori_loop(0, 1, ring_step, 0)
-    pair_step(nreq - 1, 1)
-    lax.fori_loop(1, nreq // 2, ring_step, 0)
+    cache_wait(0)
+    scores(0, sa_v, ma_v)
+    lax.fori_loop(0, nreq // 2, two_requests, 0)
+    for b in range(nreq):
+        pending['pair', b] = pair_copy(b).wait_send
+
+    direct_step(nreq - 1)
 
     def each(view, sem):
         def go(b, _):
             wait_bytes(view.at[b], sem.at[b])
             return 0
-        return lambda: lax.fori_loop(0, nreq, go, 0)
+        return lambda: lax.fori_loop(0, nring, go, 0)
 
     pending['xs_send'] = each(xsr_v, xs_send)
     pending['ys_send'] = each(ysr_v, ys_send)
     pending['ys_recv'] = each(ysr_v, ys_recv)
+    pending['rs_send'] = each(rsr_v, rs_send)
+    pending['rs_recv'] = each(rsr_v, rs_recv)
 
     done('uv')
     widen(wuv_v)
     for k in range(own):
         wv_v[k] = stage_v[pl.ds(head_in + k, latent, stride=slab), :].astype(BF16)
 
-    done('ys_recv')
-    for b in range(nreq):
-        m, l, acc = merge([ys_v[b, here[1 - b % 2]]] + [ysr_v[b, r] for r in range(side - 1)])
+    def put(b, acc, l):
         ol = rounded(acc / l)
         for k in range(own):
             olat_v[k, b:b + 1, :] = ol[k:k + 1, :]
+
+    done('ys_recv')
+    for b in range(nring):
+        m, l, acc = merge([ys_v[b, here[1 - b % 2]]] + [ysr_v[b, r] for r in range(side - 1)])
+        put(b, acc, l)
+    done('rs_recv')
+    for b in range(nring):
+        m, l, acc = merge([rs_v[b, xx * side + yy]] + [rsr_v[b, r] for r in range(chips - 1)])
+        put(nring + b, acc, l)
 
     done('wo')
     outs = []
@@ -531,14 +571,16 @@
             vm((half, latent, nope), BF16), vm((latent * 8, nope), F32),
             vm((2, nreq // 2, dmodel), F32), vm((2, nreq, qlora // 2), F32), vm((inner, nreq, wide), F32),
             vm((wide // LANES, heads * nreq, LANES), F32), vm((nreq, wide), F32),
-            vm((heads, tdev), F32), vm((heads, tdev), F32), vm((nreq, heads, LANES), F32),
+            vm((heads, tdev), F32), vm((heads, tdev), F32), vm((heads, LANES), F32), vm((heads, LANES), F32),
             vm((nreq, heads, wide), F32), vm((nreq, half, wide), F32),
-            vm((nreq, half, wide), F32), vm((nreq, side - 1, half // side, wide), F32),
-            vm((nreq, side, own, wide), F32), vm((nreq, side - 1, own, wide), F32), vm((own, nreq, latent), F32),
+            vm((nreq // 2, half, wide), F32), vm((nreq // 2, side - 1, half // side, wide), F32),
+            vm((nreq // 2, side, own, wide), F32), vm((nreq // 2, side - 1, own, wide), F32),
+            vm((nreq // 2, chips, own, wide), F32), vm((nreq // 2, chips - 1, own, wide), F32), vm((own, nreq, latent), F32),
             vm((2, nreq // 2, dmodel), F32), vm((nreq // 2, dmodel), F32),
             vm((chips, nreq // 2, tcol), F32), vm((chips - 1, nreq // 2, tcol), F32), vm((2, chips, nreq // 2, tcol), F32),
             dma((8,)), dma((dmodel // qlora,)), dma((w_uq.shape[1] // qlora,)), dma((half // 8,)), dma((2, nreq)),
-            dma, dma, dma, dma, dma((half // 8,)), dma((half // 8,)), dma((nreq,)), dma((nreq,)), dma((nreq,)), dma((nreq,)), dma((nreq,)), dma((nreq,)),
+            dma, dma, dma, dma, dma((half // 8,)), dma((half // 8,)), dma((nreq,)), dma((nreq,)), dma((nreq // 2,)), dma((nreq // 2,)), dma((nreq // 2,)), dma((nreq // 2,)),
+            dma((nreq // 2,)), dma((nreq // 2,)),
             dma, dma, dma, dma, dma, dma, dma, dma,
         ]
         packed = pl.pallas_call(

time: 59.2 us -> 55.9 us (0.944)
  Pallas kernels: 58.4 us -> 55.2 us
    pallas_call x1, Pallas kernels: 56.9 us -> 53.6 us  [decode_step(): pl.pallas_call(functools.partial(step_kernel, (cp, side)), out_shape=jax....]
where the time goes in v6:
time: 55.9 us; the launch traced here: 55.8 us
  Pallas kernels  55.2 us (99%)
  between operations  0.64 us (1%)
    pallas_call x1, Pallas kernels, decode_step(): pl.pallas_call(functools.partial(step_kernel, (cp, side)), out_shape=jax....  53.6 us
    pallas_call x1, Pallas kernels, decode_step(): pl.pallas_call(split_outputs, out_shape=out_shape, in_specs=[vspec], out_...  1.55 us

profile of v6, /device:TPU:97, one launch (start us, length us, event | category | flops | bytes accessed | tf_op | source)
XLA Modules:
  0.0 55.8 jit_solution(6275089123713040593)
XLA Ops:
  0.6 53.6 %decode_step.1.packed_v = bf16[8,6784]{1,0:T(8,128)(2,1)} custom-call(bf16[8,6144]{1,0:T(8,128)(2,1)} %x_h.1, bf16[6144,1536]{1,0:T(8,128)(2,1)} %wdq_h.1, f32[1536]{0:T(1024)} %gq_h.1, bf16[1536,12288]{1,0:T(8,128)(2,1)} %wuq_h.1, bf16[576,6144]{1,0:T(8,128)(2,1)} %bitcast.3, f32[1,512]{1,0:T(1,128)} %bitcast.5, bf16[512,64,128]{2,1,0:T(8,128)(2,1)} %wuk_h.1, ...), custom_call_target="tpu_custom_call" | custom-call | tf_op jit(solution)/shard_map/decode_step/pallas_call | solution.py:586
  54.3 1.5 %split_outputs.1 = (bf16[8,6144]{1,0:T(8,128)(2,1)}, bf16[8,512]{1,0:T(8,128)(2,1)}, bf16[8,64]{1,0:T(8,128)(2,1)}) custom-call(bf16[8,6784]{1,0:T(8,128)(2,1)} %decode_step.1.packed_v), custom_call_target="tpu_custom_call" | custom-call | tf_op jit(solution)/shard_map/split_outputs/pallas_call | solution.py:597

commit v7 on v6

--- a/solution.py
+++ b/solution.py
@@ -480,8 +480,9 @@
     for b in range(nring):
         m, l, acc = merge([ys_v[b, here[1 - b % 2]]] + [ysr_v[b, r] for r in range(side - 1)])
         put(b, acc, l)
-    done('rs_recv')
+    pending.pop('rs_recv')
     for b in range(nring):
+        wait_bytes(rsr_v.at[b], rs_recv.at[b])
         m, l, acc = merge([rs_v[b, xx * side + yy]] + [rsr_v[b, r] for r in range(chips - 1)])
         put(nring + b, acc, l)
 
@@ -490,15 +491,21 @@
     for k in range(own):
         outs.append(dot(olat_v[k].astype(BF16), wv_v[k]).astype(BF16))
     o = jnp.concatenate(outs, axis=1)
-    ncol = 768
-    for j in range(dmodel // ncol):
+    ncol = dmodel // 8
+
+    def po_copy(k):
+        cols = pl.ds(k * (dmodel // 2), dmodel // 2)
+        return pltpu.make_async_remote_copy(src_ref=po_v.at[oc, :, cols], dst_ref=pop_v.at[:, cols], send_sem=po_send.at[k],
+                                            recv_sem=po_recv.at[k], device_id={'cp': partner}, device_id_type=MESH)
+
+    for j in range(8):
         pj = dot(o, wo_v[:, j * ncol:(j + 1) * ncol])
         for i in range(2):
             po_v[i, :, j * ncol:(j + 1) * ncol] = pj[4 * i:4 * i + 4, :]
-    po_copy = pltpu.make_async_remote_copy(src_ref=po_v.at[oc], dst_ref=pop_v, send_sem=po_send, recv_sem=po_recv,
-                                           device_id={'cp': partner}, device_id_type=MESH)
-    po_copy.start()
-    po_copy.wait()
+        if j % 4 == 3:
+            po_copy(j // 4).start()
+    for k in range(2):
+        po_copy(k).wait()
     tcol = dmodel // chips
     for k in range(chips):
         pt_v[k] = po_v[c, :, k * tcol:(k + 1) * tcol] + pop_v[:, k * tcol:(k + 1) * tcol]
@@ -581,7 +588,7 @@
             dma((8,)), dma((dmodel // qlora,)), dma((w_uq.shape[1] // qlora,)), dma((half // 8,)), dma((2, nreq)),
             dma, dma, dma, dma, dma((half // 8,)), dma((half // 8,)), dma((nreq,)), dma((nreq,)), dma((nreq // 2,)), dma((nreq // 2,)), dma((nreq // 2,)), dma((nreq // 2,)),
             dma((nreq // 2,)), dma((nreq // 2,)),
-            dma, dma, dma, dma, dma, dma, dma, dma,
+            dma((2,)), dma((2,)), dma, dma, dma, dma, dma, dma,
         ]
         packed = pl.pallas_call(
             functools.partial(step_kernel, (cp, side)),

time: 55.9 us -> 55.9 us (level)
  no operation moved by 1% of the time
where the time goes in v7:
time: 55.9 us; the launch traced here: 55.7 us
  Pallas kernels  55.1 us (99%)
  between operations  0.64 us (1%)
    pallas_call x1, Pallas kernels, decode_step(): pl.pallas_call(functools.partial(step_kernel, (cp, side)), out_shape=jax....  53.5 us
    pallas_call x1, Pallas kernels, decode_step(): pl.pallas_call(split_outputs, out_shape=out_shape, in_specs=[vspec], out_...  1.55 us

profile of v7, /device:TPU:97, one launch (start us, length us, event | category | flops | bytes accessed | tf_op | source)
XLA Modules:
  0.0 55.7 jit_solution(9379855391403067087)
XLA Ops:
  0.6 53.5 %decode_step.1.packed_v = bf16[8,6784]{1,0:T(8,128)(2,1)} custom-call(bf16[8,6144]{1,0:T(8,128)(2,1)} %x_h.1, bf16[6144,1536]{1,0:T(8,128)(2,1)} %wdq_h.1, f32[1536]{0:T(1024)} %gq_h.1, bf16[1536,12288]{1,0:T(8,128)(2,1)} %wuq_h.1, bf16[576,6144]{1,0:T(8,128)(2,1)} %bitcast.3, f32[1,512]{1,0:T(1,128)} %bitcast.5, bf16[512,64,128]{2,1,0:T(8,128)(2,1)} %wuk_h.1, ...), custom_call_target="tpu_custom_call" | custom-call | tf_op jit(solution)/shard_map/decode_step/pallas_call | solution.py:593
  54.2 1.5 %split_outputs.1 = (bf16[8,6144]{1,0:T(8,128)(2,1)}, bf16[8,512]{1,0:T(8,128)(2,1)}, bf16[8,64]{1,0:T(8,128)(2,1)}) custom-call(bf16[8,6784]{1,0:T(8,128)(2,1)} %decode_step.1.packed_v), custom_call_target="tpu_custom_call" | custom-call | tf_op jit(solution)/shard_map/split_outputs/pallas_call | solution.py:604
